TPU v7x, 128 devices: a whole 4x4x4 slice. The times are simulated.
128 devices in a mesh: blk: 16 (over y, z), tm: 8 (over x, core).
Axes of the slice: x: 4, y: 4, z: 4, core: 2. Of those that a mesh axis runs over, the one named last changes fastest.
Arguments:
- solution: float32 [512, 128, 1024], P('blk', 'tm'), may hold values from -6 to 6
- residual: float32 [512, 128, 1024], P('blk', 'tm'), may hold values from -12 to 12
- direction: float32 [512, 128, 1024], P('blk', 'tm'), may hold values from -6 to 6
- noise_var: float32 [512, 128, 1024], P('blk', 'tm'), may hold values from 0.5 to 2
- legendre: bfloat16 [512, 512, 512], P('blk', 'tm'), may hold values from -0.25 to 0.25
- temporal: float32 [512, 128, 128], P('tm'), may hold values from -3 to 3.5, as said below
- order_table: int32 [512], replicated, may hold values from 0 to 511, as said below
Outputs:
- solution_new: float32 [512, 128, 1024], P('blk', 'tm')
- residual_new: float32 [512, 128, 1024], P('blk', 'tm')
- direction_new: float32 [512, 128, 1024], P('blk', 'tm')
Inputs may be any that keep to these rules, and one draw needn't show every extreme that they name: `order_table`: each value 0 to 511 appears once. In each aligned block of 32 entries, entry 16 + k equals 511 minus entry k, so each block holds pairs of orders m and 511 - m. `temporal`: each matrix is symmetric and positive definite.
All inputs are finite; a program needn't handle non-finite values.
Results may differ from a plain program's by a relative error of at most 0.0048.
Values may be sent and summed in bfloat16 or wider, within the bound.
A program may use at most 192 MiB of HBM per device.

v0:
```python
import math

import jax
import jax.numpy as jnp
from jax import lax
from jax.experimental import pallas as pl
from jax.experimental.pallas import tpu as pltpu
from jax.sharding import Mesh
from jax.sharding import PartitionSpec as P

BLK = ("blk_0", "blk_1")
TM = ("tm_0", "tm_1")
BLK_TM = ("blk_0", "blk_1", "tm_0", "tm_1")
BF = jnp.bfloat16
F32 = jnp.float32
MESH = pl.DeviceIdType.MESH
GROUPS = 4
ORD = 8
VM = pl.BlockSpec(memory_space=pltpu.VMEM)


def unit_circle(phase):
    quadrant = (phase + 128) // 256
    x = (phase - quadrant * 256).astype(F32) * (2.0 * math.pi / 1024)
    x2 = x * x
    s = x * (1.0 + x2 * (-1.0 / 6 + x2 * (1.0 / 120 + x2 * (-1.0 / 5040 + x2 / 362880))))
    c = 1.0 + x2 * (-0.5 + x2 * (1.0 / 24 + x2 * (-1.0 / 720 + x2 / 40320)))
    odd = quadrant % 2 == 1
    cos = jnp.where(odd, s, c)
    sin = jnp.where(odd, c, s)
    cos = jnp.where((quadrant == 1) | (quadrant == 2), -cos, cos)
    sin = jnp.where((quadrant == 2) | (quadrant == 3), -sin, sin)
    return cos, sin


def table_dft_kernel(orders, direction, table, spectra, rows, split):
    lat, time = 32, 16
    lane = lax.broadcasted_iota(jnp.int32, (ORD, 128), 1)
    scale = 1.0 / math.sqrt(512.0)

    for q in range(8):
        split[q * 512 : (q + 1) * 512, :] = direction[:, q * 128 : (q + 1) * 128]

    def gather(t, _):
        for q in range(8):
            rows[pl.ds(pl.multiple_of(t * lat, lat), lat), q * 128 : (q + 1) * 128] = split[
                pl.ds(q * 512 + t, lat, stride=time), :
            ].astype(BF)
        return 0

    lax.fori_loop(0, time, gather, 0)

    def fill(n, _):
        m = orders[pl.ds(pl.multiple_of(n * ORD, ORD), ORD), :]
        cos, sin = unit_circle((m * lane) % 1024)
        turn_c, turn_s = unit_circle((m * 128) % 1024)
        cos, sin = cos * scale, sin * scale
        for q in range(8):
            table[pl.ds(pl.multiple_of(n * 16, 16), 16), q * 128 : (q + 1) * 128] = (
                jnp.concatenate([cos, sin], axis=0).astype(BF)
            )
            cos, sin = cos * turn_c - sin * turn_s, sin * turn_c + cos * turn_s
        return 0

    lax.fori_loop(0, 64, fill, 0)

    def transform(n, _):
        part = lax.dot_general(
            table[pl.ds(pl.multiple_of(n * 256, 256), 256), :],
            rows[...],
            (((1,), (1,)), ((), ())),
            preferred_element_type=F32,
        )
        spectra[pl.ds(n * 4, 4)] = part.astype(BF).reshape(4, GROUPS, 2 * ORD, 512)
        return 0

    lax.fori_loop(0, 4, transform, 0)


def table_dft(orders, direction):
    return pl.pallas_call(
        table_dft_kernel,
        out_shape=(
            jax.ShapeDtypeStruct((1024, 1024), BF),
            jax.ShapeDtypeStruct((16, GROUPS, 2 * ORD, 512), BF),
        ),
        in_specs=[VM, VM],
        out_specs=(VM, VM),
        scratch_shapes=[pltpu.VMEM((512, 1024), BF), pltpu.VMEM((4096, 128), F32)],
        compiler_params=pltpu.CompilerParams(vmem_limit_bytes=40 * 1024 * 1024),
        name="table_dft",
    )(orders, direction)


def lane_swap():
    row = lax.broadcasted_iota(jnp.int32, (512, 512), 0)
    col = lax.broadcasted_iota(jnp.int32, (512, 512), 1)
    moved = (row // 32 % 4) * 128 + (row // 128) * 32 + row % 32
    return (col == moved).astype(F32).astype(BF)


def front_kernel(spectra, full, recv, mid, perm, a2a_send, a2a_recv, own_send, fwd_send, peer_send,
                 line_recv, far_recv, peer_recv):
    y, z = lax.axis_index("blk_0"), lax.axis_index("blk_1")
    x, core = lax.axis_index("tm_0"), lax.axis_index("tm_1")
    me = y * 4 + z
    right, left, far = (x + 1) % 4, (x + 3) % 4, (x + 2) % 4
    barrier = pltpu.get_barrier_semaphore()

    def greet(k, _):
        pl.semaphore_signal(
            barrier, inc=1, device_id={"blk_0": (y + k // 4) % 4, "blk_1": (z + k % 4) % 4},
            device_id_type=MESH,
        )
        return 0

    lax.fori_loop(1, 16, greet, 0)
    pl.semaphore_signal(barrier, inc=1, device_id={"tm_0": right}, device_id_type=MESH)
    pl.semaphore_signal(barrier, inc=1, device_id={"tm_0": left}, device_id_type=MESH)
    pl.semaphore_signal(barrier, inc=1, device_id={"tm_1": 1 - core}, device_id_type=MESH)
    perm[...] = lane_swap()
    pl.semaphore_wait(barrier, 18)

    def block_copy(g, k):
        ty, tz = (y + k // 4) % 4, (z + k % 4) % 4
        return pltpu.make_async_remote_copy(
            src_ref=spectra.at[ty * 4 + tz, g], dst_ref=recv.at[g, me],
            send_sem=a2a_send.at[g, k], recv_sem=a2a_recv.at[g, k],
            device_id={"blk_0": ty, "blk_1": tz}, device_id_type=MESH,
        )

    def send_block(n, _):
        block_copy(n // 15, n % 15 + 1).start()
        return 0

    lax.fori_loop(0, GROUPS * 15, send_block, 0)
    for g in range(GROUPS):
        recv[g, pl.ds(me, 1)] = spectra[pl.ds(me, 1), g]

    def part(g, plane, who, first, count):
        return full.at[pl.ds(g * ORD + first, count), :, pl.ds(pl.multiple_of((plane * 2 + who) * 16, 16), 16), :]

    def line_copy(g, way):
        ref = part(g, x, core, 0, ORD)
        return pltpu.make_async_remote_copy(
            src_ref=ref, dst_ref=ref, send_sem=own_send.at[g, way], recv_sem=line_recv.at[g, way],
            device_id={"tm_0": right if way == 0 else left}, device_id_type=MESH,
        )

    def far_copy(g, way):
        ref = part(g, left if way == 0 else right, core, way * (ORD // 2), ORD // 2)
        return pltpu.make_async_remote_copy(
            src_ref=ref, dst_ref=ref, send_sem=fwd_send.at[g, way], recv_sem=far_recv.at[g, way],
            device_id={"tm_0": right if way == 0 else left}, device_id_type=MESH,
        )

    def peer_copy(g, slot):
        plane, first, count = (
            (x, 0, ORD), (left, 0, ORD), (right, 0, ORD), (far, 0, ORD // 2), (far, ORD // 2, ORD // 2)
        )[slot]
        ref = part(g, plane, core, first, count)
        return pltpu.make_async_remote_copy(
            src_ref=ref, dst_ref=ref, send_sem=peer_send.at[g, slot], recv_sem=peer_recv.at[g, slot],
            device_id={"tm_1": 1 - core}, device_id_type=MESH,
        )

    def regroup(g):
        rows = []
        for sq in range(4):
            for tq in range(4):
                rows.append(jnp.concatenate(
                    [recv[g, sq * 4 + s, :, tq * 128 : (tq + 1) * 128] for s in range(4)], axis=1))
        moved = jnp.dot(jnp.concatenate(rows, axis=0), perm[...], preferred_element_type=F32)
        for sq in range(4):
            for tq in range(4):
                n = (sq * 4 + tq) * 16
                for t in range(4):
                    m = sq * 256 + (tq * 4 + t) * 16
                    mid[m : m + 16, :] = moved[n : n + 16, t * 128 : (t + 1) * 128]
        for c in range(2):
            for i in range(ORD):
                for sq in range(4):
                    full[g * ORD + i, c, pl.ds(pl.multiple_of((x * 2 + core) * 16, 16), 16),
                         sq * 128 : (sq + 1) * 128] = (
                        mid[pl.ds(sq * 256 + c * ORD + i, 16, stride=16), :].astype(BF))

    for g in range(GROUPS + 2):
        if g < GROUPS:
            def arrive(k, _):
                block_copy(g, k).wait_recv()
                return 0

            lax.fori_loop(1, 16, arrive, 0)
            regroup(g)
            line_copy(g, 0).start()
            line_copy(g, 1).start()
            peer_copy(g, 0).start()
        if 1 <= g <= GROUPS:
            line_copy(g - 1, 0).wait_recv()
            far_copy(g - 1, 0).start()
            peer_copy(g - 1, 1).start()
            line_copy(g - 1, 1).wait_recv()
            far_copy(g - 1, 1).start()
            peer_copy(g - 1, 2).start()
        if g >= 2:
            far_copy(g - 2, 0).wait_recv()
            peer_copy(g - 2, 3).start()
            far_copy(g - 2, 1).wait_recv()
            peer_copy(g - 2, 4).start()
    for g in range(GROUPS):
        for slot in range(5):
            peer_copy(g, slot).wait_recv()
    for g in range(GROUPS):
        for slot in range(5):
            peer_copy(g, slot).wait_send()
        for way in range(2):
            line_copy(g, way).wait_send()
            far_copy(g, way).wait_send()

    def sent(n, _):
        block_copy(n // 15, n % 15 + 1).wait_send()
        return 0

    lax.fori_loop(0, GROUPS * 15, sent, 0)


def front(spectra):
    dma = pltpu.SemaphoreType.DMA
    return pl.pallas_call(
        front_kernel,
        out_shape=jax.ShapeDtypeStruct((32, 2, 128, 512), BF),
        in_specs=[VM],
        out_specs=VM,
        scratch_shapes=[
            pltpu.VMEM((GROUPS, 16, 2 * ORD, 512), BF),
            pltpu.VMEM((1024, 128), F32),
            pltpu.VMEM((512, 512), BF),
            dma((GROUPS, 16)), dma((GROUPS, 16)),
            dma((GROUPS, 2)), dma((GROUPS, 2)), dma((GROUPS, 5)),
            dma((GROUPS, 2)), dma((GROUPS, 2)), dma((GROUPS, 5)),
        ],
        compiler_params=pltpu.CompilerParams(
            collective_id=0, has_side_effects=True, vmem_limit_bytes=40 * 1024 * 1024),
        name="front",
    )(spectra)


def order_groups(order_table):
    pairs = order_table.reshape(16, 2, 16)[:, 0]
    low = jnp.minimum(pairs, 511 - pairs)
    both = jnp.stack([low, 511 - low], axis=1).reshape(16, 2, 2, ORD)
    return jnp.broadcast_to(both.reshape(512, 1), (512, 128))


def back_kernel(part, out, acc, far_in, fin_in, blocks, mid, perm, peer_send, peer_recv, far_send,
                far_recv, line_send, line_recv, a2a_send, a2a_recv):
    y, z = lax.axis_index("blk_0"), lax.axis_index("blk_1")
    x, core = lax.axis_index("tm_0"), lax.axis_index("tm_1")
    me = y * 4 + z
    right, left, far = (x + 1) % 4, (x + 3) % 4, (x + 2) % 4
    half = ORD // 2
    barrier = pltpu.get_barrier_semaphore()

    def greet(k, _):
        pl.semaphore_signal(
            barrier, inc=1, device_id={"blk_0": (y + k // 4) % 4, "blk_1": (z + k % 4) % 4},
            device_id_type=MESH,
        )
        return 0

    lax.fori_loop(1, 16, greet, 0)
    pl.semaphore_signal(barrier, inc=1, device_id={"tm_0": right}, device_id_type=MESH)
    pl.semaphore_signal(barrier, inc=1, device_id={"tm_0": left}, device_id_type=MESH)
    pl.semaphore_signal(barrier, inc=1, device_id={"tm_1": 1 - core}, device_id_type=MESH)
    perm[...] = lane_swap()
    pl.semaphore_wait(barrier, 18)
    planes = (far, right, left, x)

    def hours(plane, who):
        return pl.ds(pl.multiple_of((plane * 2 + who) * 16, 16), 16)

    def peer_copy(g, n):
        return pltpu.make_async_remote_copy(
            src_ref=part.at[pl.ds(g * ORD, ORD), :, hours(planes[n], 1 - core), :],
            dst_ref=acc.at[g, n],
            send_sem=peer_send.at[g, n], recv_sem=peer_recv.at[g, n],
            device_id={"tm_1": 1 - core}, device_id_type=MESH,
        )

    def far_copy(g, way):
        return pltpu.make_async_remote_copy(
            src_ref=acc.at[g, 0, pl.ds(way * half, half)], dst_ref=far_in.at[g, way],
            send_sem=far_send.at[g, way], recv_sem=far_recv.at[g, way],
            device_id={"tm_0": right if way == 0 else left}, device_id_type=MESH,
        )

    def line_copy(g, way):
        return pltpu.make_async_remote_copy(
            src_ref=acc.at[g, 1 + way], dst_ref=fin_in.at[g, way],
            send_sem=line_send.at[g, way], recv_sem=line_recv.at[g, way],
            device_id={"tm_0": right if way == 0 else left}, device_id_type=MESH,
        )

    def block_copy(g, k):
        ty, tz = (y + k // 4) % 4, (z + k % 4) % 4
        return pltpu.make_async_remote_copy(
            src_ref=blocks.at[g, ty * 4 + tz], dst_ref=out.at[me, g],
            send_sem=a2a_send.at[g, k], recv_sem=a2a_recv.at[g, k],
            device_id={"blk_0": ty, "blk_1": tz}, device_id_type=MESH,
        )

    def add_own(g, n):
        def step(i, _):
            own = part[g * ORD + i, :, hours(planes[n], core), :]
            acc[g, n, i] = (acc[g, n, i].astype(F32) + own.astype(F32)).astype(BF)
            return 0

        lax.fori_loop(0, ORD, step, 0)

    def add_far(g, way):
        def step(i, _):
            acc[g, 1 + way, way * half + i] = (
                acc[g, 1 + way, way * half + i].astype(F32) + far_in[g, way, i].astype(F32)
            ).astype(BF)
            return 0

        lax.fori_loop(0, half, step, 0)

    def regroup(g):
        for i in range(ORD):
            for c in range(2):
                total = (acc[g, 3, i, c].astype(F32) + fin_in[g, 0, i, c].astype(F32)
                         + fin_in[g, 1, i, c].astype(F32))
                for sq in range(4):
                    mid[pl.ds(sq * 256 + c * ORD + i, 16, stride=16), :] = (
                        total[:, sq * 128 : (sq + 1) * 128])
        rows = []
        for sq in range(4):
            for tq in range(4):
                m = sq * 256 + tq * 64
                rows.append(jnp.concatenate(
                    [mid[m + t * 16 : m + (t + 1) * 16, :].astype(BF) for t in range(4)], axis=1))
        moved = jnp.dot(
            jnp.concatenate(rows, axis=0), perm[...], preferred_element_type=F32).astype(BF)
        for sq in range(4):
            for tq in range(4):
                n = (sq * 4 + tq) * 16
                for s in range(4):
                    blocks[g, sq * 4 + s, :, tq * 128 : (tq + 1) * 128] = (
                        moved[n : n + 16, s * 128 : (s + 1) * 128])

    for g in range(GROUPS):
        for n in range(4):
            peer_copy(g, n).start()
    for g in range(GROUPS + 2):
        if g < GROUPS:
            for n in range(4):
                peer_copy(g, n).wait_recv()
                add_own(g, n)
                if n == 0:
                    far_copy(g, 0).start()
                    far_copy(g, 1).start()
        if 1 <= g <= GROUPS:
            for way in range(2):
                far_copy(g - 1, way).wait_recv()
                add_far(g - 1, way)
                line_copy(g - 1, way).start()
        if g >= 2:
            line_copy(g - 2, 0).wait_recv()
            line_copy(g - 2, 1).wait_recv()
            regroup(g - 2)

            def send_block(k, _):
                block_copy(g - 2, k).start()
                return 0

            lax.fori_loop(1, 16, send_block, 0)
            out[pl.ds(me, 1), g - 2] = blocks[g - 2, pl.ds(me, 1)]
    for g in range(GROUPS):
        for n in range(4):
            peer_copy(g, n).wait_send()
        for way in range(2):
            far_copy(g, way).wait_send()
            line_copy(g, way).wait_send()

    def finish(n, _):
        block_copy(n // 15, n % 15 + 1).wait_recv()
        block_copy(n // 15, n % 15 + 1).wait_send()
        return 0

    lax.fori_loop(0, GROUPS * 15, finish, 0)


def back(part):
    dma = pltpu.SemaphoreType.DMA
    return pl.pallas_call(
        back_kernel,
        out_shape=jax.ShapeDtypeStruct((16, GROUPS, 2 * ORD, 512), BF),
        in_specs=[VM],
        out_specs=VM,
        scratch_shapes=[
            pltpu.VMEM((GROUPS, 4, ORD, 2, 16, 512), BF),
            pltpu.VMEM((GROUPS, 2, ORD // 2, 2, 16, 512), BF),
            pltpu.VMEM((GROUPS, 2, ORD, 2, 16, 512), BF),
            pltpu.VMEM((GROUPS, 16, 2 * ORD, 512), BF),
            pltpu.VMEM((1024, 128), F32),
            pltpu.VMEM((512, 512), BF),
            dma((GROUPS, 4)), dma((GROUPS, 4)), dma((GROUPS, 2)), dma((GROUPS, 2)),
            dma((GROUPS, 2)), dma((GROUPS, 2)), dma((GROUPS, 16)), dma((GROUPS, 16)),
        ],
        compiler_params=pltpu.CompilerParams(
            collective_id=1, has_side_effects=True, vmem_limit_bytes=48 * 1024 * 1024),
        name="back",
    )(part)


def product_kernel(entries, table, residual, direction, noise, product, sums, split, stage, line,
                   plane, line_send, line_recv, plane_send, plane_recv):
    y, z = lax.axis_index("blk_0"), lax.axis_index("blk_1")
    x, core = lax.axis_index("tm_0"), lax.axis_index("tm_1")
    row, col = y * 4 + z, x * 2 + core

    def in_line(k):
        return {"tm_0": (x + k // 2) % 4, "tm_1": (core + k) % 2}

    def in_plane(k):
        return {"blk_0": (y + k // 4) % 4, "blk_1": (z + k % 4) % 4}

    barrier = pltpu.get_barrier_semaphore()

    def greet_line(k, _):
        pl.semaphore_signal(barrier, inc=1, device_id=in_line(k), device_id_type=MESH)
        return 0

    def greet_plane(k, _):
        pl.semaphore_signal(barrier, inc=1, device_id=in_plane(k), device_id_type=MESH)
        return 0

    lax.fori_loop(1, 8, greet_line, 0)
    lax.fori_loop(1, 16, greet_plane, 0)

    def synthesis(n, _):
        cols = entries[:, pl.ds(pl.multiple_of(n * 128, 128), 128)]
        block = lax.dot_general(cols, table[...], (((0,), (0,)), ((), ())), preferred_element_type=F32)
        for t in range(4):
            for q in range(8):
                split[pl.ds(q * 512 + n * 4 + t, 32, stride=16), :] = (
                    block[t * 32 : (t + 1) * 32, q * 128 : (q + 1) * 128])
        return 0

    lax.fori_loop(0, 4, synthesis, 0)

    def combine(n, totals):
        rows = pl.ds(pl.multiple_of(n * 8, 8), 8)
        nn, dp, rp, pp = totals
        for q in range(8):
            cols = slice(q * 128, (q + 1) * 128)
            d, r = direction[rows, cols], residual[rows, cols]
            p = split[pl.ds(pl.multiple_of(q * 512 + n * 8, 8), 8), :] + noise[rows, cols] * d
            product[rows, cols] = p
            nn, dp, rp, pp = nn + r * r, dp + d * p, rp + r * p, pp + p * p
        return nn, dp, rp, pp

    zero = jnp.zeros((8, 128), F32)
    totals = lax.fori_loop(0, 64, combine, (zero, zero, zero, zero))
    for k in range(4):
        stage[0, 2 * k : 2 * k + 2, :] = jnp.broadcast_to(
            jnp.sum(totals[k], axis=0, keepdims=True), (2, 128))
    pl.semaphore_wait(barrier, 22)

    def line_copy(k):
        return pltpu.make_async_remote_copy(
            src_ref=stage.at[0], dst_ref=line.at[col], send_sem=line_send.at[k],
            recv_sem=line_recv.at[k], device_id=in_line(k), device_id_type=MESH)

    def plane_copy(k):
        return pltpu.make_async_remote_copy(
            src_ref=stage.at[1], dst_ref=plane.at[row], send_sem=plane_send.at[k],
            recv_sem=plane_recv.at[k], device_id=in_plane(k), device_id_type=MESH)

    for k in range(1, 8):
        line_copy(k).start()
    line[pl.ds(col, 1)] = stage[0:1]
    for k in range(1, 8):
        line_copy(k).wait_recv()
    stage[1] = jnp.sum(line[...], axis=0)
    for k in range(1, 16):
        plane_copy(k).start()
    plane[pl.ds(row, 1)] = stage[1:2]
    for k in range(1, 16):
        plane_copy(k).wait_recv()
    sums[...] = jnp.sum(plane[...], axis=0)
    for k in range(1, 8):
        line_copy(k).wait_send()
    for k in range(1, 16):
        plane_copy(k).wait_send()


def product_sums(entries, table, residual, direction, noise):
    dma = pltpu.SemaphoreType.DMA
    return pl.pallas_call(
        product_kernel,
        out_shape=(jax.ShapeDtypeStruct((512, 1024), F32), jax.ShapeDtypeStruct((8, 128), F32)),
        in_specs=[VM] * 5,
        out_specs=(VM, VM),
        scratch_shapes=[
            pltpu.VMEM((4096, 128), F32),
            pltpu.VMEM((2, 8, 128), F32),
            pltpu.VMEM((8, 8, 128), F32),
            pltpu.VMEM((16, 8, 128), F32),
            dma((8,)), dma((8,)), dma((16,)), dma((16,)),
        ],
        compiler_params=pltpu.CompilerParams(
            collective_id=2, has_side_effects=True, vmem_limit_bytes=48 * 1024 * 1024),
        name="product_sums",
    )(entries, table, residual, direction, noise)


def update_kernel(sums, solution, residual, direction, product, solution_new, residual_new,
                  direction_new):
    def total(k):
        return jnp.sum(sums[2 * k : 2 * k + 1, :], axis=1, keepdims=True)

    norm_now, curvature, cross, square = total(0), total(1), total(2), total(3)
    step = norm_now / curvature
    norm_next = norm_now - 2.0 * step * cross + step * step * square
    ratio = norm_next / norm_now
    d = direction[...]
    r = residual[...] - step * product[...]
    solution_new[...] = solution[...] + step * d
    residual_new[...] = r
    direction_new[...] = r + ratio * d


def update(sums, solution, residual, direction, product):
    block = pl.BlockSpec((64, 1024), lambda n: (n, 0))
    shape = jax.ShapeDtypeStruct((512, 1024), F32)
    return pl.pallas_call(
        update_kernel,
        grid=(8,),
        out_shape=(shape, shape, shape),
        in_specs=[pl.BlockSpec((8, 128), lambda n: (0, 0))] + [block] * 4,
        out_specs=(block, block, block),
        name="update",
    )(sums, solution, residual, direction, product)


def body(solution, residual, direction, noise_var, legendre, temporal, order_table):
    per_device, deg_dev, lat_all = legendre.shape
    shape = direction.shape
    flat = lambda v: v.reshape(512, 1024)
    groups = order_groups(order_table)
    table, spectra = table_dft(groups, flat(direction))
    cycles = front(spectra)
    own = lax.dynamic_slice_in_dim(order_table, lax.axis_index(BLK) * per_device, per_device)
    degrees = lax.axis_index(TM) * deg_dev + jnp.arange(deg_dev, dtype=jnp.int32)
    low_first = (own[:16] < 256)[:, None, None]
    first, second = legendre[:16], legendre[16:]
    low = jnp.minimum(own[:16], 511 - own[:16])
    orders = jnp.concatenate([low, 511 - low])
    swapped = jnp.concatenate(
        [jnp.where(low_first, first, second), jnp.where(low_first, second, first)], axis=0)
    masked = jnp.where(degrees[None, :, None] >= orders[:, None, None], swapped, jnp.zeros_like(swapped))
    coeffs = jnp.einsum(
        "icta,ila->lict", cycles, masked, preferred_element_type=F32).astype(BF)
    mixed = jnp.einsum(
        "lict,ltu->licu", coeffs, temporal.astype(BF), preferred_element_type=F32).astype(BF)
    terms = jnp.einsum("ila,licu->icua", masked, mixed, preferred_element_type=F32).astype(BF)
    entries = back(terms).reshape(1024, 512)
    product, sums = product_sums(entries, table, flat(residual), flat(direction), flat(noise_var))
    outs = update(sums, flat(solution), flat(residual), flat(direction), product)
    return tuple(o.reshape(shape) for o in outs)


def solution(mesh):
    torus = Mesh(mesh.devices.reshape(4, 4, 4, 2), ("blk_0", "blk_1", "tm_0", "tm_1"))
    return jax.shard_map(
        body,
        mesh=torus,
        in_specs=(
            P(BLK, TM, None),
            P(BLK, TM, None),
            P(BLK, TM, None),
            P(BLK, TM, None),
            P(BLK, TM, None),
            P(TM, None, None),
            P(),
        ),
        out_specs=(P(BLK, TM, None), P(BLK, TM, None), P(BLK, TM, None)),
        check_vma=False,
    )
```

profile of v0, /device:TPU:1, one launch (start us, length us, event | category | flops | bytes accessed | tf_op | source)
XLA Modules:
  0.0 154.0 jit_solution(8846642511853079972)
XLA Ops:
  0.6 0.8 dynamic_slice.3
  1.4 0.1 pad_add_fusion.1
  1.5 0.1 broadcast_compare_fusion
  1.6 0.8 reshape.75
  2.4 0.1 broadcast_in_dim.35
  2.5 0.1 broadcast_in_dim.36.orders
  2.6 0.0 copy-start
  2.6 1.9 %broadcast_select_fusion.1 = (bf16[16,64,512]{2,1,0:T(8,128)(2,1)S(1)}, bf16[16,64,512]{2,1,0:T(8,128)(2,1)S(1)}) fusion(pred[16]{0:T(512)(128)(4,1)S(1)} %slice_compare_fusion, bf16[32,64,512]{2,1,0:T(8,128)(2,1)} %param.11), kind=kLoop, calls=%fused_computation.12 | loop fusion | flops 1048576 | bytes 4194320 | tf_op jit(solution)/shard_map/jit(_where)/select_n | solution.py:562
  4.5 0.3 copy-done
  4.9 6.6 %table_dft.1 = (bf16[1024,1024]{1,0:T(8,128)(2,1)S(1)}, bf16[16,4,16,512]{3,2,1,0:T(8,128)(2,1)S(1)}) custom-call(s32[512,128]{1,0:T(8,128)S(1)} %broadcast_in_dim.36.orders, f32[512,1024]{1,0:T(8,128)S(1)} %bitcast.27), custom_call_target="tpu_custom_call" | custom-call | tf_op jit(solution)/shard_map/table_dft/pallas_call | solution.py:81
  11.5 55.1 %front.1 = bf16[32,2,128,512]{3,2,1,0:T(8,128)(2,1)S(1)} custom-call(bf16[16,4,16,512]{3,2,1,0:T(8,128)(2,1)S(1)} %get-tuple-element.10.spectra), custom_call_target="tpu_custom_call" | custom-call | tf_op jit(solution)/shard_map/front/pallas_call | solution.py:229
  66.6 0.0 copy-start.3
  66.6 2.8 %fusion.7 = bf16[64,32,2,128]{3,0,2,1:T(8,128)(2,1)S(1)} fusion(bf16[32,2,128,512]{3,2,1,0:T(8,128)(2,1)S(1)} %front.1, bf16[16,64,512]{2,1,0:T(8,128)(2,1)S(1)} %get-tuple-element.18, bf16[16,64,512]{2,1,0:T(8,128)(2,1)S(1)} %get-tuple-element.17, pred[32,64]{1,0:T(8,128)(4,1)S(1)} %broadcast_compare_fusion), kind=kOutput, calls=%fused_computation.8 | convolution fusion | flops 542638080 | bytes 11536384 | tf_op jit(solution)/shard_map/icta,ila->lict/dot_general | solution.py:564
  69.5 0.0 copy-done.3
  69.5 1.2 fusion.4
  70.7 4.9 %convolution_convert_fusion.part = bf16[32,2,128,512]{3,2,1,0:T(8,128)(2,1)} fusion(bf16[64,32,2,128]{3,1,2,0:T(8,128)(2,1)S(1)} %fusion.4, bf16[16,64,512]{2,1,0:T(8,128)(2,1)S(1)} %get-tuple-element.18, bf16[16,64,512]{2,1,0:T(8,128)(2,1)S(1)} %get-tuple-element.17, pred[32,64]{1,0:T(8,128)(4,1)S(1)} %broadcast_compare_fusion), kind=kOutput, calls=%fused_computation | convolution fusion | flops 543162368 | bytes 11536384 | tf_op jit(solution)/shard_map/ila,licu->icua/dot_general | solution.py:568
  75.7 51.8 %back.1 = bf16[16,4,16,512]{3,2,1,0:T(8,128)(2,1)S(1)} custom-call(bf16[32,2,128,512]{3,2,1,0:T(8,128)(2,1)} %convolution_convert_fusion.part), custom_call_target="tpu_custom_call" | custom-call | tf_op jit(solution)/shard_map/back/pallas_call | solution.py:396
  127.5 16.1 %product_sums.1 = (f32[512,1024]{1,0:T(8,128)S(1)}, f32[8,128]{1,0:T(8,128)S(1)}) custom-call(bf16[1024,512]{1,0:T(8,128)(2,1)S(1)} %bitcast.28, bf16[1024,1024]{1,0:T(8,128)(2,1)S(1)} %get-tuple-element.11.table, f32[512,1024]{1,0:T(8,128)} %bitcast.29, f32[512,1024]{1,0:T(8,128)} %bitcast.25, f32[512,1024]{1,0:T(8,128)} %bitcast.31), custom_call_target="tpu_custom_call" | custom-call | tf_op jit(solution)/shard_map/product_sums/pallas_call | solution.py:501
  143.7 0.0 copy-start.1
  143.7 1.3 copy-done.1
  145.0 0.0 copy-start.2
  145.0 0.6 copy-done.2
  145.6 8.4 %update.1 = (f32[512,1024]{1,0:T(8,128)}, f32[512,1024]{1,0:T(8,128)}, f32[512,1024]{1,0:T(8,128)}) custom-call(f32[8,128]{1,0:T(8,128)} %copy-done.2, f32[512,1024]{1,0:T(8,128)} %bitcast.32, f32[512,1024]{1,0:T(8,128)} %bitcast.30, f32[512,1024]{1,0:T(8,128)} %bitcast.26, f32[512,1024]{1,0:T(8,128)} %copy-done.1), custom_call_target="tpu_custom_call" | custom-call | tf_op jit(solution)/shard_map/update/pallas_call | solution.py:538
  (7 shorter events, 0.0 us)
Async XLA Ops:
  2.6 2.2 %copy-start = (f32[32,16,1024]{2,1,0:T(8,128)S(1)}, f32[32,16,1024]{2,1,0:T(8,128)}, u32[]{:S(2)}) copy-start(f32[32,16,1024]{2,1,0:T(8,128)} %param.9) | copy-start | bytes 6291460
  66.6 2.9 %copy-start.3 = (f32[64,128,128]{2,1,0:T(8,128)S(1)}, f32[64,128,128]{2,1,0:T(8,128)}, u32[]{:S(2)}) copy-start(f32[64,128,128]{2,1,0:T(8,128)} %param.12) | copy-start | bytes 12582916
  143.7 1.3 copy-start.1
  145.0 0.6 copy-start.2
where the time goes:
time: 154 us
  Pallas kernels  138 us (90%)
  matrix products  9.01 us (6%)
  local copies, waits for them, and re-layouts  4.01 us (3%)
  other arithmetic  2.07 us (1%)
    pallas_call x1, Pallas kernels, front(): pl.pallas_call(front_kernel, out_shape=jax.ShapeDtypeStruct((32, 2, 128,...  55.1 us
    pallas_call x1, Pallas kernels, back(): pl.pallas_call(back_kernel, out_shape=jax.ShapeDtypeStruct((16, GROUPS, 2...  51.8 us
    pallas_call x1, Pallas kernels, product_sums(): pl.pallas_call(product_kernel, out_shape=(jax.ShapeDtypeStruct((512, 1024...  16.1 us
    pallas_call x1, Pallas kernels, update(): pl.pallas_call(update_kernel, grid=(8,), out_shape=(shape, shape, shape),...  8.37 us
    pallas_call x1, Pallas kernels, table_dft(): pl.pallas_call(table_dft_kernel, out_shape=(jax.ShapeDtypeStruct((1024, 1...  6.62 us
    dot_general x1, matrix products, body(): jnp.einsum('ila,licu->icua', masked, mixed, preferred_element_type=F32)  4.94 us

commit v1 on v0

v1 whole, which is shorter than its diff:
```python
import math

import jax
import jax.numpy as jnp
from jax import lax
from jax.experimental import pallas as pl
from jax.experimental.pallas import tpu as pltpu
from jax.sharding import Mesh
from jax.sharding import PartitionSpec as P

BLK = ("blk_0", "blk_1")
TM = ("tm_0", "tm_1")
BLK_TM = ("blk_0", "blk_1", "tm_0", "tm_1")
BF = jnp.bfloat16
F32 = jnp.float32
MESH = pl.DeviceIdType.MESH
GROUPS = 4
ORD = 8
VM = pl.BlockSpec(memory_space=pltpu.VMEM)


def unit_circle(phase):
    quadrant = (phase + 128) // 256
    x = (phase - quadrant * 256).astype(F32) * (2.0 * math.pi / 1024)
    x2 = x * x
    s = x * (1.0 + x2 * (-1.0 / 6 + x2 * (1.0 / 120 + x2 * (-1.0 / 5040 + x2 / 362880))))
    c = 1.0 + x2 * (-0.5 + x2 * (1.0 / 24 + x2 * (-1.0 / 720 + x2 / 40320)))
    odd = quadrant % 2 == 1
    cos = jnp.where(odd, s, c)
    sin = jnp.where(odd, c, s)
    cos = jnp.where((quadrant == 1) | (quadrant == 2), -cos, cos)
    sin = jnp.where((quadrant == 2) | (quadrant == 3), -sin, sin)
    return cos, sin


def table_dft_kernel(orders, direction, table, spectra, rows, split):
    lat, time = 32, 16
    lane = lax.broadcasted_iota(jnp.int32, (ORD, 128), 1)
    scale = 1.0 / math.sqrt(512.0)

    for q in range(8):
        split[q * 512 : (q + 1) * 512, :] = direction[:, q * 128 : (q + 1) * 128]

    def gather(t, _):
        for q in range(8):
            rows[pl.ds(pl.multiple_of(t * lat, lat), lat), q * 128 : (q + 1) * 128] = split[
                pl.ds(q * 512 + t, lat, stride=time), :
            ].astype(BF)
        return 0

    lax.fori_loop(0, time, gather, 0)

    def fill(n, _):
        m = orders[pl.ds(pl.multiple_of(n * ORD, ORD), ORD), :]
        cos, sin = unit_circle((m * lane) % 1024)
        turn_c, turn_s = unit_circle((m * 128) % 1024)
        cos, sin = cos * scale, sin * scale
        for q in range(8):
            table[pl.ds(pl.multiple_of(n * 16, 16), 16), q * 128 : (q + 1) * 128] = (
                jnp.concatenate([cos, sin], axis=0).astype(BF)
            )
            cos, sin = cos * turn_c - sin * turn_s, sin * turn_c + cos * turn_s
        return 0

    lax.fori_loop(0, 64, fill, 0)

    def transform(n, _):
        part = lax.dot_general(
            table[pl.ds(pl.multiple_of(n * 256, 256), 256), :],
            rows[...],
            (((1,), (1,)), ((), ())),
            preferred_element_type=F32,
        )
        spectra[pl.ds(n * 4, 4)] = part.astype(BF).reshape(4, GROUPS, 2 * ORD, 512)
        return 0

    lax.fori_loop(0, 4, transform, 0)


def table_dft(orders, direction):
    return pl.pallas_call(
        table_dft_kernel,
        out_shape=(
            jax.ShapeDtypeStruct((1024, 1024), BF),
            jax.ShapeDtypeStruct((16, GROUPS, 2 * ORD, 512), BF),
        ),
        in_specs=[VM, VM],
        out_specs=(VM, VM),
        scratch_shapes=[pltpu.VMEM((512, 1024), BF), pltpu.VMEM((4096, 128), F32)],
        compiler_params=pltpu.CompilerParams(vmem_limit_bytes=40 * 1024 * 1024),
        name="table_dft",
    )(orders, direction)


def lane_swap():
    row = lax.broadcasted_iota(jnp.int32, (512, 512), 0)
    col = lax.broadcasted_iota(jnp.int32, (512, 512), 1)
    moved = (row // 32 % 4) * 128 + (row // 128) * 32 + row % 32
    return (col == moved).astype(F32).astype(BF)


def order_groups(order_table):
    pairs = order_table.reshape(16, 2, 16)[:, 0]
    low = jnp.minimum(pairs, 511 - pairs)
    swap = jnp.where(pairs == low, 0, 1024)
    both = jnp.stack([low + swap, 511 - low + swap], axis=1).reshape(512, 1)
    return jnp.broadcast_to(both, (512, 128))


def core_kernel(spectra, orders, legendre, temporal, out, full, part, leg, recv, blocks, mid, perm,
                coef, mixed, acc, far_in, fin_in, in_send, in_recv, own_send, fwd_send, dup_send,
                own_recv, fwd_recv, dup_recv, pair_send, pair_recv, far_send, far_recv, line_send,
                line_recv, out_send, out_recv):
    y, z = lax.axis_index("blk_0"), lax.axis_index("blk_1")
    x, core = lax.axis_index("tm_0"), lax.axis_index("tm_1")
    me = y * 4 + z
    right, left, far = (x + 1) % 4, (x + 3) % 4, (x + 2) % 4
    half = ORD // 2
    barrier = pltpu.get_barrier_semaphore()

    def greet(k, _):
        pl.semaphore_signal(
            barrier, inc=1, device_id={"blk_0": (y + k // 4) % 4, "blk_1": (z + k % 4) % 4},
            device_id_type=MESH,
        )
        return 0

    lax.fori_loop(1, 16, greet, 0)
    pl.semaphore_signal(barrier, inc=1, device_id={"tm_0": right}, device_id_type=MESH)
    pl.semaphore_signal(barrier, inc=1, device_id={"tm_0": left}, device_id_type=MESH)
    pl.semaphore_signal(barrier, inc=1, device_id={"tm_1": 1 - core}, device_id_type=MESH)
    pl.semaphore_wait(barrier, 18)
    side = ({"tm_0": right}, {"tm_0": left})
    peer = {"tm_1": 1 - core}

    def remote(src, dst, send, recv_sem, device):
        return pltpu.make_async_remote_copy(
            src_ref=src, dst_ref=dst, send_sem=send, recv_sem=recv_sem, device_id=device,
            device_id_type=MESH)

    def in_copy(g, k):
        ty, tz = (y + k // 4) % 4, (z + k % 4) % 4
        return remote(spectra.at[ty * 4 + tz, g], recv.at[g, me], in_send.at[g, k],
                      in_recv.at[g, k], {"blk_0": ty, "blk_1": tz})

    def out_copy(g, k):
        ty, tz = (y + k // 4) % 4, (z + k % 4) % 4
        return remote(blocks.at[g, ty * 4 + tz], out.at[me, g], out_send.at[g, k],
                      out_recv.at[g, k], {"blk_0": ty, "blk_1": tz})

    def hours(plane, who):
        return pl.ds(pl.multiple_of((plane * 2 + who) * 16, 16), 16)

    def piece(g, plane, first, count):
        return full.at[pl.ds(g * ORD + first, count), :, hours(plane, core), :]

    def own_copy(g, way):
        ref = piece(g, x, 0, ORD)
        return remote(ref, ref, own_send.at[g, way], own_recv.at[g, way], side[way])

    def fwd_copy(g, way):
        ref = piece(g, left if way == 0 else right, way * half, half)
        return remote(ref, ref, fwd_send.at[g, way], fwd_recv.at[g, way], side[way])

    def dup_copy(g, slot):
        plane, first, count = (
            (x, 0, ORD), (left, 0, ORD), (right, 0, ORD), (far, 0, half), (far, half, half))[slot]
        ref = piece(g, plane, first, count)
        return remote(ref, ref, dup_send.at[g, slot], dup_recv.at[g, slot], peer)

    planes = (far, right, left, x)

    def pair_copy(g, n):
        return remote(part.at[pl.ds(g * ORD, ORD), :, hours(planes[n], 1 - core), :], acc.at[g, n],
                      pair_send.at[g, n], pair_recv.at[g, n], peer)

    def far_copy(g, way):
        return remote(acc.at[g, 0, pl.ds(way * half, half)], far_in.at[g, way],
                      far_send.at[g, way], far_recv.at[g, way], side[way])

    def line_copy(g, way):
        return remote(acc.at[g, 1 + way], fin_in.at[g, way], line_send.at[g, way],
                      line_recv.at[g, way], side[way])

    def arrive(g):
        def wait(k, _):
            in_copy(g, k).wait_recv()
            return 0

        lax.fori_loop(1, 16, wait, 0)
        rows = []
        for sq in range(4):
            for tq in range(4):
                rows.append(jnp.concatenate(
                    [recv[g, sq * 4 + s, :, tq * 128 : (tq + 1) * 128] for s in range(4)], axis=1))
        moved = jnp.dot(jnp.concatenate(rows, axis=0), perm[...], preferred_element_type=F32)
        for sq in range(4):
            for tq in range(4):
                n = (sq * 4 + tq) * 16
                for t in range(4):
                    m = sq * 256 + (tq * 4 + t) * 16
                    mid[m : m + 16, :] = moved[n : n + 16, t * 128 : (t + 1) * 128]
        for c in range(2):
            for i in range(ORD):
                for sq in range(4):
                    full[g * ORD + i, c, hours(x, core), sq * 128 : (sq + 1) * 128] = (
                        mid[pl.ds(sq * 256 + c * ORD + i, 16, stride=16), :].astype(BF))
        own_copy(g, 0).start()
        own_copy(g, 1).start()
        dup_copy(g, 0).start()

    def forward(g):
        for way in range(2):
            own_copy(g, way).wait_recv()
            fwd_copy(g, way).start()
            dup_copy(g, 1 + way).start()

    def forward_far(g):
        for way in range(2):
            fwd_copy(g, way).wait_recv()
            dup_copy(g, 3 + way).start()

    def middle(g):
        for slot in range(5):
            dup_copy(g, slot).wait_recv()

        def analyse(i, _):
            value = lax.dot_general(
                leg[g * ORD + i], full[g * ORD + i].reshape(256, 512), (((1,), (1,)), ((), ())),
                preferred_element_type=F32)
            row = pl.multiple_of(i * 64, 64)
            coef[pl.ds(row, 64), :] = value[:, :128]
            coef[pl.ds(ORD * 64 + row, 64), :] = value[:, 128:]
            return 0

        lax.fori_loop(0, ORD, analyse, 0, unroll=2)

        def mix(n, _):
            for k in range(16):
                l = n * 16 + k
                rows = jnp.concatenate(
                    [coef[pl.ds(c * ORD * 64 + l, ORD, stride=64), :] for c in range(2)], axis=0)
                mixed[pl.ds(pl.multiple_of(l * 16, 16), 16), :] = jnp.dot(
                    rows.astype(BF), temporal[l].astype(BF), preferred_element_type=F32)
            return 0

        lax.fori_loop(0, 4, mix, 0)

        def synthesise(i, _):
            rows = jnp.concatenate(
                [mixed[pl.ds(c * ORD + i, 64, stride=16), :] for c in range(2)], axis=1)
            value = lax.dot_general(
                rows.astype(BF), leg[g * ORD + i], (((0,), (0,)), ((), ())),
                preferred_element_type=F32)
            part[g * ORD + i] = value.astype(BF).reshape(2, 128, 512)
            return 0

        lax.fori_loop(0, ORD, synthesise, 0, unroll=2)
        for n in range(4):
            pair_copy(g, n).start()

    def add_pair(g):
        for n in range(4):
            pair_copy(g, n).wait_recv()

            def step(i, _):
                own = part[g * ORD + i, :, hours(planes[n], core), :]
                acc[g, n, i] = (acc[g, n, i].astype(F32) + own.astype(F32)).astype(BF)
                return 0

            lax.fori_loop(0, ORD, step, 0)
            if n == 0:
                far_copy(g, 0).start()
                far_copy(g, 1).start()

    def add_far(g):
        for way in range(2):
            far_copy(g, way).wait_recv()

            def step(i, _):
                acc[g, 1 + way, way * half + i] = (
                    acc[g, 1 + way, way * half + i].astype(F32) + far_in[g, way, i].astype(F32)
                ).astype(BF)
                return 0

            lax.fori_loop(0, half, step, 0)
            line_copy(g, way).start()

    def depart(g):
        line_copy(g, 0).wait_recv()
        line_copy(g, 1).wait_recv()
        for i in range(ORD):
            for c in range(2):
                total = (acc[g, 3, i, c].astype(F32) + fin_in[g, 0, i, c].astype(F32)
                         + fin_in[g, 1, i, c].astype(F32))
                for sq in range(4):
                    mid[pl.ds(sq * 256 + c * ORD + i, 16, stride=16), :] = (
                        total[:, sq * 128 : (sq + 1) * 128])
        rows = []
        for sq in range(4):
            for tq in range(4):
                m = sq * 256 + tq * 64
                rows.append(jnp.concatenate(
                    [mid[m + t * 16 : m + (t + 1) * 16, :].astype(BF) for t in range(4)], axis=1))
        moved = jnp.dot(
            jnp.concatenate(rows, axis=0), perm[...], preferred_element_type=F32).astype(BF)
        for sq in range(4):
            for tq in range(4):
                n = (sq * 4 + tq) * 16
                for s in range(4):
                    blocks[g, sq * 4 + s, :, tq * 128 : (tq + 1) * 128] = (
                        moved[n : n + 16, s * 128 : (s + 1) * 128])

        def send(k, _):
            out_copy(g, k).start()
            return 0

        lax.fori_loop(1, 16, send, 0)
        out[pl.ds(me, 1), g] = blocks[g, pl.ds(me, 1)]

    def send_in(n, _):
        in_copy(n // 15, n % 15 + 1).start()
        return 0

    lax.fori_loop(0, GROUPS * 15, send_in, 0)
    for g in range(GROUPS):
        recv[g, pl.ds(me, 1)] = spectra[pl.ds(me, 1), g]
    perm[...] = lane_swap()
    degree = (x * 2 + core) * 64 + lax.broadcasted_iota(jnp.int32, (64, 512), 0)

    def mask(k, _):
        both = (legendre[k].astype(F32), legendre[16 + k].astype(F32))
        for h in range(2):
            entry = jnp.concatenate([orders[pl.ds(me * 32 + h * 16 + k, 1), :]] * 4, axis=1)
            entry = jnp.broadcast_to(entry, (64, 512))
            row = jnp.where(entry >= 1024, both[1 - h], both[h])
            leg[h * 16 + k] = jnp.where(degree >= entry % 1024, row, 0.0).astype(BF)
        return 0

    lax.fori_loop(0, 16, mask, 0)
    arrive(0)
    arrive(1)
    forward(0)
    arrive(2)
    forward(1)
    forward_far(0)
    arrive(3)
    middle(0)
    forward(2)
    forward_far(1)
    add_pair(0)
    middle(1)
    forward(3)
    add_pair(1)
    forward_far(2)
    middle(2)
    add_far(0)
    add_pair(2)
    forward_far(3)
    middle(3)
    add_far(1)
    add_pair(3)
    depart(0)
    add_far(2)
    depart(1)
    add_far(3)
    depart(2)
    depart(3)
    for g in range(GROUPS):
        for slot in range(5):
            dup_copy(g, slot).wait_send()
        for n in range(4):
            pair_copy(g, n).wait_send()
        for way in range(2):
            own_copy(g, way).wait_send()
            fwd_copy(g, way).wait_send()
            far_copy(g, way).wait_send()
            line_copy(g, way).wait_send()

    def finish(n, _):
        in_copy(n // 15, n % 15 + 1).wait_send()
        out_copy(n // 15, n % 15 + 1).wait_recv()
        out_copy(n // 15, n % 15 + 1).wait_send()
        return 0

    lax.fori_loop(0, GROUPS * 15, finish, 0)


def core_stage(spectra, orders, legendre, temporal):
    dma = pltpu.SemaphoreType.DMA
    two, four, five, blk = dma((GROUPS, 2)), dma((GROUPS, 4)), dma((GROUPS, 5)), dma((GROUPS, 16))
    return pl.pallas_call(
        core_kernel,
        out_shape=jax.ShapeDtypeStruct((16, GROUPS, 2 * ORD, 512), BF),
        in_specs=[VM] * 4,
        out_specs=VM,
        scratch_shapes=[
            pltpu.VMEM((32, 2, 128, 512), BF),
            pltpu.VMEM((32, 2, 128, 512), BF),
            pltpu.VMEM((32, 64, 512), BF),
            pltpu.VMEM((GROUPS, 16, 2 * ORD, 512), BF),
            pltpu.VMEM((GROUPS, 16, 2 * ORD, 512), BF),
            pltpu.VMEM((1024, 128), F32),
            pltpu.VMEM((512, 512), BF),
            pltpu.VMEM((2 * ORD * 64, 128), F32),
            pltpu.VMEM((2 * ORD * 64, 128), F32),
            pltpu.VMEM((GROUPS, 4, ORD, 2, 16, 512), BF),
            pltpu.VMEM((GROUPS, 2, ORD // 2, 2, 16, 512), BF),
            pltpu.VMEM((GROUPS, 2, ORD, 2, 16, 512), BF),
            blk, blk, two, two, five, two, two, five, four, four, two, two, two, two, blk, blk,
        ],
        compiler_params=pltpu.CompilerParams(
            collective_id=0, has_side_effects=True, vmem_limit_bytes=48 * 1024 * 1024),
        name="core_stage",
    )(spectra, orders, legendre, temporal)


def product_kernel(entries, table, residual, direction, noise, product, sums, split, stage, line,
                   plane, line_send, line_recv, plane_send, plane_recv):
    y, z = lax.axis_index("blk_0"), lax.axis_index("blk_1")
    x, core = lax.axis_index("tm_0"), lax.axis_index("tm_1")
    row, col = y * 4 + z, x * 2 + core

    def in_line(k):
        return {"tm_0": (x + k // 2) % 4, "tm_1": (core + k) % 2}

    def in_plane(k):
        return {"blk_0": (y + k // 4) % 4, "blk_1": (z + k % 4) % 4}

    barrier = pltpu.get_barrier_semaphore()

    def greet_line(k, _):
        pl.semaphore_signal(barrier, inc=1, device_id=in_line(k), device_id_type=MESH)
        return 0

    def greet_plane(k, _):
        pl.semaphore_signal(barrier, inc=1, device_id=in_plane(k), device_id_type=MESH)
        return 0

    lax.fori_loop(1, 8, greet_line, 0)
    lax.fori_loop(1, 16, greet_plane, 0)

    def synthesis(n, _):
        cols = entries[:, pl.ds(pl.multiple_of(n * 128, 128), 128)]
        block = lax.dot_general(cols, table[...], (((0,), (0,)), ((), ())), preferred_element_type=F32)
        for t in range(4):
            for q in range(8):
                split[pl.ds(q * 512 + n * 4 + t, 32, stride=16), :] = (
                    block[t * 32 : (t + 1) * 32, q * 128 : (q + 1) * 128])
        return 0

    lax.fori_loop(0, 4, synthesis, 0)

    def combine(n, totals):
        rows = pl.ds(pl.multiple_of(n * 8, 8), 8)
        nn, dp, rp, pp = totals
        for q in range(8):
            cols = slice(q * 128, (q + 1) * 128)
            d, r = direction[rows, cols], residual[rows, cols]
            p = split[pl.ds(pl.multiple_of(q * 512 + n * 8, 8), 8), :] + noise[rows, cols] * d
            product[rows, cols] = p
            nn, dp, rp, pp = nn + r * r, dp + d * p, rp + r * p, pp + p * p
        return nn, dp, rp, pp

    zero = jnp.zeros((8, 128), F32)
    totals = lax.fori_loop(0, 64, combine, (zero, zero, zero, zero))
    for k in range(4):
        stage[0, 2 * k : 2 * k + 2, :] = jnp.broadcast_to(
            jnp.sum(totals[k], axis=0, keepdims=True), (2, 128))
    pl.semaphore_wait(barrier, 22)

    def line_copy(k):
        return pltpu.make_async_remote_copy(
            src_ref=stage.at[0], dst_ref=line.at[col], send_sem=line_send.at[k],
            recv_sem=line_recv.at[k], device_id=in_line(k), device_id_type=MESH)

    def plane_copy(k):
        return pltpu.make_async_remote_copy(
            src_ref=stage.at[1], dst_ref=plane.at[row], send_sem=plane_send.at[k],
            recv_sem=plane_recv.at[k], device_id=in_plane(k), device_id_type=MESH)

    for k in range(1, 8):
        line_copy(k).start()
    line[pl.ds(col, 1)] = stage[0:1]
    for k in range(1, 8):
        line_copy(k).wait_recv()
    stage[1] = jnp.sum(line[...], axis=0)
    for k in range(1, 16):
        plane_copy(k).start()
    plane[pl.ds(row, 1)] = stage[1:2]
    for k in range(1, 16):
        plane_copy(k).wait_recv()
    sums[...] = jnp.sum(plane[...], axis=0)
    for k in range(1, 8):
        line_copy(k).wait_send()
    for k in range(1, 16):
        plane_copy(k).wait_send()


def product_sums(entries, table, residual, direction, noise):
    dma = pltpu.SemaphoreType.DMA
    return pl.pallas_call(
        product_kernel,
        out_shape=(jax.ShapeDtypeStruct((512, 1024), F32), jax.ShapeDtypeStruct((8, 128), F32)),
        in_specs=[VM] * 5,
        out_specs=(VM, VM),
        scratch_shapes=[
            pltpu.VMEM((4096, 128), F32),
            pltpu.VMEM((2, 8, 128), F32),
            pltpu.VMEM((8, 8, 128), F32),
            pltpu.VMEM((16, 8, 128), F32),
            dma((8,)), dma((8,)), dma((16,)), dma((16,)),
        ],
        compiler_params=pltpu.CompilerParams(
            collective_id=2, has_side_effects=True, vmem_limit_bytes=48 * 1024 * 1024),
        name="product_sums",
    )(entries, table, residual, direction, noise)


def update_kernel(sums, solution, residual, direction, product, solution_new, residual_new,
                  direction_new, stage, sems):
    def total(k):
        return jnp.sum(sums[2 * k : 2 * k + 1, :], axis=1, keepdims=True)

    norm_now, curvature, cross, square = total(0), total(1), total(2), total(3)
    step = norm_now / curvature
    norm_next = norm_now - 2.0 * step * cross + step * step * square
    ratio = norm_next / norm_now
    outs = (solution_new, residual_new, direction_new)

    def copy(n, k):
        rows = pl.ds(pl.multiple_of(n * 64, 64), 64)
        return pltpu.make_async_copy(stage.at[k, rows, :], outs[k].at[rows, :], sems.at[n, k])

    def block(n, _):
        rows = pl.ds(pl.multiple_of(n * 64, 64), 64)
        d = direction[rows, :]
        r = residual[rows, :] - step * product[rows, :]
        stage[0, rows, :] = solution[rows, :] + step * d
        stage[1, rows, :] = r
        stage[2, rows, :] = r + ratio * d
        for k in range(3):
            copy(n, k).start()
        return 0

    lax.fori_loop(0, 8, block, 0)

    def drain(n, _):
        for k in range(3):
            copy(n, k).wait()
        return 0

    lax.fori_loop(0, 8, drain, 0)


def update(sums, solution, residual, direction, product):
    shape = jax.ShapeDtypeStruct((512, 1024), F32)
    hbm = pl.BlockSpec(memory_space=pl.ANY)
    return pl.pallas_call(
        update_kernel,
        out_shape=(shape, shape, shape),
        in_specs=[VM] * 5,
        out_specs=(hbm, hbm, hbm),
        scratch_shapes=[pltpu.VMEM((3, 512, 1024), F32), pltpu.SemaphoreType.DMA((8, 3))],
        compiler_params=pltpu.CompilerParams(vmem_limit_bytes=24 * 1024 * 1024),
        name="update",
    )(sums, solution, residual, direction, product)


def body(solution, residual, direction, noise_var, legendre, temporal, order_table):
    shape = direction.shape
    flat = lambda v: v.reshape(512, 1024)
    orders = order_groups(order_table)
    table, spectra = table_dft(orders, flat(direction))
    entries = core_stage(spectra, orders, legendre, temporal).reshape(1024, 512)
    product, sums = product_sums(entries, table, flat(residual), flat(direction), flat(noise_var))
    outs = update(sums, flat(solution), flat(residual), flat(direction), product)
    return tuple(o.reshape(shape) for o in outs)


def solution(mesh):
    torus = Mesh(mesh.devices.reshape(4, 4, 4, 2), ("blk_0", "blk_1", "tm_0", "tm_1"))
    return jax.shard_map(
        body,
        mesh=torus,
        in_specs=(
            P(BLK, TM, None),
            P(BLK, TM, None),
            P(BLK, TM, None),
            P(BLK, TM, None),
            P(BLK, TM, None),
            P(TM, None, None),
            P(),
        ),
        out_specs=(P(BLK, TM, None), P(BLK, TM, None), P(BLK, TM, None)),
        check_vma=False,
    )
```

time: 154 us -> 125 us (0.81)
  Pallas kernels: 138 us -> 122 us
  matrix products: 9.01 us -> 0 us
  other arithmetic: 2.07 us -> 0.04 us
    pallas_call x3 -> x2, Pallas kernels: 115 us -> 99.1 us  [the longest x1 96.1 us: core_stage(): pl.pallas_call(core_kernel, out_shape=jax.ShapeDtypeStruct((16, GROUPS, 2...]
    dot_general x3 -> x0, matrix products: 9.01 us -> none  [the longest x1 4.94 us: body(): jnp.einsum('ila,licu->icua', masked, mixed, preferred_element_type=F32)]
    select_n x1 -> x0, other arithmetic: 1.89 us -> none  [body(): jnp.where(low_first, first, second)]
where the time goes in v1:
time: 125 us
  Pallas kernels  122 us (98%)
  local copies, waits for them, and re-layouts  2.6 us (2%)
    pallas_call x1, Pallas kernels, core_stage(): pl.pallas_call(core_kernel, out_shape=jax.ShapeDtypeStruct((16, GROUPS, 2...  96.1 us
    pallas_call x1, Pallas kernels, product_sums(): pl.pallas_call(product_kernel, out_shape=(jax.ShapeDtypeStruct((512, 1024...  16.2 us
    pallas_call x1, Pallas kernels, table_dft(): pl.pallas_call(table_dft_kernel, out_shape=(jax.ShapeDtypeStruct((1024, 1...  6.65 us
    pallas_call x1, Pallas kernels, update(): pl.pallas_call(update_kernel, out_shape=(shape, shape, shape), in_specs=[...  3 us

profile of v1, /device:TPU:1, one launch (start us, length us, event | category | flops | bytes accessed | tf_op | source)
XLA Modules:
  0.0 125.3 jit_solution(5122572994005297347)
XLA Ops:
  0.6 0.8 reshape.38
  1.5 0.1 broadcast_in_dim.17
  1.6 0.1 broadcast_in_dim.18.orders
  1.7 0.0 copy-start
  1.7 1.6 %copy-done = f32[32,16,1024]{2,1,0:T(8,128)S(1)} copy-done((f32[32,16,1024]{2,1,0:T(8,128)S(1)}, f32[32,16,1024]{2,1,0:T(8,128)}, u32[]{:S(2)}) %copy-start) | copy-done | bytes 2097176
  3.3 0.0 copy-start.3
  3.3 6.6 %table_dft.1 = (bf16[1024,1024]{1,0:T(8,128)(2,1)S(1)}, bf16[16,4,16,512]{3,2,1,0:T(8,128)(2,1)S(1)}) custom-call(s32[512,128]{1,0:T(8,128)S(1)} %broadcast_in_dim.18.orders, f32[512,1024]{1,0:T(8,128)S(1)} %bitcast.9), custom_call_target="tpu_custom_call" | custom-call | tf_op jit(solution)/shard_map/table_dft/pallas_call | solution.py:81
  9.9 0.0 copy-done.3
  10.0 96.1 %core_stage.1 = bf16[16,4,16,512]{3,2,1,0:T(8,128)(2,1)S(1)} custom-call(bf16[16,4,16,512]{3,2,1,0:T(8,128)(2,1)S(1)} %get-tuple-element.10.spectra, s32[512,128]{1,0:T(8,128)S(1)} %broadcast_in_dim.18.orders, bf16[32,64,512]{2,1,0:T(8,128)(2,1)S(1)} %copy-done.3, f32[64,128,128]{2,1,0:T(8,128)} %temporal.1), custom_call_target="tpu_custom_call" | custom-call | tf_op jit(solution)/shard_map/core_stage/pallas_call | solution.py:392
  106.0 0.0 copy-start.1
  106.0 0.0 copy-start.2
  106.1 0.0 copy-start.4
  106.1 16.2 %product_sums.1 = (f32[512,1024]{1,0:T(8,128)S(1)}, f32[8,128]{1,0:T(8,128)S(1)}) custom-call(bf16[1024,512]{1,0:T(8,128)(2,1)S(1)} %bitcast.13, bf16[1024,1024]{1,0:T(8,128)(2,1)S(1)} %get-tuple-element.11.table, f32[512,1024]{1,0:T(8,128)} %bitcast.11, f32[512,1024]{1,0:T(8,128)} %bitcast.8, f32[512,1024]{1,0:T(8,128)} %bitcast.15), custom_call_target="tpu_custom_call" | custom-call | tf_op jit(solution)/shard_map/product_sums/pallas_call | solution.py:502
  122.3 0.0 copy-done.1
  122.3 0.0 copy-done.2
  122.3 0.0 copy-done.4
  122.3 3.0 %update.1 = (f32[512,1024]{1,0:T(8,128)}, f32[512,1024]{1,0:T(8,128)}, f32[512,1024]{1,0:T(8,128)}) custom-call(f32[8,128]{1,0:T(8,128)S(1)} %get-tuple-element.12.sums, f32[512,1024]{1,0:T(8,128)S(1)} %bitcast.14, f32[512,1024]{1,0:T(8,128)S(1)} %bitcast.12, f32[512,1024]{1,0:T(8,128)S(1)} %bitcast.10, f32[512,1024]{1,0:T(8,128)S(1)} %get-tuple-element.13.product), custom_call_target="tpu_custom_call" | custom-call | tf_op jit(solution)/shard_map/update/pallas_call | solution.py:559
  (2 shorter events, 0.0 us)
Async XLA Ops:
  1.7 1.6 %copy-start = (f32[32,16,1024]{2,1,0:T(8,128)S(1)}, f32[32,16,1024]{2,1,0:T(8,128)}, u32[]{:S(2)}) copy-start(f32[32,16,1024]{2,1,0:T(8,128)} %param.9) | copy-start | bytes 6291460
  3.3 6.7 %copy-start.3 = (bf16[32,64,512]{2,1,0:T(8,128)(2,1)S(1)}, bf16[32,64,512]{2,1,0:T(8,128)(2,1)}, u32[]{:S(2)}) copy-start(bf16[32,64,512]{2,1,0:T(8,128)(2,1)} %legendre.1) | copy-start | bytes 6291460
  106.0 16.2 %copy-start.1 = (f32[32,16,1024]{2,1,0:T(8,128)S(1)}, f32[32,16,1024]{2,1,0:T(8,128)}, u32[]{:S(2)}) copy-start(f32[32,16,1024]{2,1,0:T(8,128)} %param.9) | copy-start | bytes 6291460
  106.0 16.2 %copy-start.2 = (f32[32,16,1024]{2,1,0:T(8,128)S(1)}, f32[32,16,1024]{2,1,0:T(8,128)}, u32[]{:S(2)}) copy-start(f32[32,16,1024]{2,1,0:T(8,128)} %param.8) | copy-start | bytes 6291460
  106.1 16.2 %copy-start.4 = (f32[32,16,1024]{2,1,0:T(8,128)S(1)}, f32[32,16,1024]{2,1,0:T(8,128)}, u32[]{:S(2)}) copy-start(f32[32,16,1024]{2,1,0:T(8,128)} %param.7) | copy-start | bytes 6291460

commit v2 on v1

--- a/solution.py
+++ b/solution.py
@@ -33,65 +33,6 @@
     return cos, sin
 
 
-def table_dft_kernel(orders, direction, table, spectra, rows, split):
-    lat, time = 32, 16
-    lane = lax.broadcasted_iota(jnp.int32, (ORD, 128), 1)
-    scale = 1.0 / math.sqrt(512.0)
-
-    for q in range(8):
-        split[q * 512 : (q + 1) * 512, :] = direction[:, q * 128 : (q + 1) * 128]
-
-    def gather(t, _):
-        for q in range(8):
-            rows[pl.ds(pl.multiple_of(t * lat, lat), lat), q * 128 : (q + 1) * 128] = split[
-                pl.ds(q * 512 + t, lat, stride=time), :
-            ].astype(BF)
-        return 0
-
-    lax.fori_loop(0, time, gather, 0)
-
-    def fill(n, _):
-        m = orders[pl.ds(pl.multiple_of(n * ORD, ORD), ORD), :]
-        cos, sin = unit_circle((m * lane) % 1024)
-        turn_c, turn_s = unit_circle((m * 128) % 1024)
-        cos, sin = cos * scale, sin * scale
-        for q in range(8):
-            table[pl.ds(pl.multiple_of(n * 16, 16), 16), q * 128 : (q + 1) * 128] = (
-                jnp.concatenate([cos, sin], axis=0).astype(BF)
-            )
-            cos, sin = cos * turn_c - sin * turn_s, sin * turn_c + cos * turn_s
-        return 0
-
-    lax.fori_loop(0, 64, fill, 0)
-
-    def transform(n, _):
-        part = lax.dot_general(
-            table[pl.ds(pl.multiple_of(n * 256, 256), 256), :],
-            rows[...],
-            (((1,), (1,)), ((), ())),
-            preferred_element_type=F32,
-        )
-        spectra[pl.ds(n * 4, 4)] = part.astype(BF).reshape(4, GROUPS, 2 * ORD, 512)
-        return 0
-
-    lax.fori_loop(0, 4, transform, 0)
-
-
-def table_dft(orders, direction):
-    return pl.pallas_call(
-        table_dft_kernel,
-        out_shape=(
-            jax.ShapeDtypeStruct((1024, 1024), BF),
-            jax.ShapeDtypeStruct((16, GROUPS, 2 * ORD, 512), BF),
-        ),
-        in_specs=[VM, VM],
-        out_specs=(VM, VM),
-        scratch_shapes=[pltpu.VMEM((512, 1024), BF), pltpu.VMEM((4096, 128), F32)],
-        compiler_params=pltpu.CompilerParams(vmem_limit_bytes=40 * 1024 * 1024),
-        name="table_dft",
-    )(orders, direction)
-
-
 def lane_swap():
     row = lax.broadcasted_iota(jnp.int32, (512, 512), 0)
     col = lax.broadcasted_iota(jnp.int32, (512, 512), 1)
@@ -99,18 +40,20 @@
     return (col == moved).astype(F32).astype(BF)
 
 
-def order_groups(order_table):
-    pairs = order_table.reshape(16, 2, 16)[:, 0]
-    low = jnp.minimum(pairs, 511 - pairs)
-    swap = jnp.where(pairs == low, 0, 1024)
-    both = jnp.stack([low + swap, 511 - low + swap], axis=1).reshape(512, 1)
-    return jnp.broadcast_to(both, (512, 128))
-
-
-def core_kernel(spectra, orders, legendre, temporal, out, full, part, leg, recv, blocks, mid, perm,
-                coef, mixed, acc, far_in, fin_in, in_send, in_recv, own_send, fwd_send, dup_send,
+def step_kernel(orders, direction_in, residual_in, noise_in, legendre_in, temporal_in, product, sums,
+                direction, residual, noise, legendre, temporal, load, split, rows, table, spectra,
+                full, part, leg, recv, blocks, mid, perm, coef, mixed, acc, far_in, fin_in, out, synth,
+                stage, line, plane, in_send, in_recv, own_send, fwd_send, dup_send,
                 own_recv, fwd_recv, dup_recv, pair_send, pair_recv, far_send, far_recv, line_send,
-                line_recv, out_send, out_recv):
+                line_recv, out_send, out_recv, sum_send, sum_recv, all_send, all_recv):
+    loads = [
+        pltpu.make_async_copy(src, dst, load.at[n])
+        for n, (src, dst) in enumerate((
+            (direction_in, direction), (legendre_in, legendre), (temporal_in, temporal),
+            (residual_in, residual), (noise_in, noise)))
+    ]
+    for copy in loads:
+        copy.start()
     y, z = lax.axis_index("blk_0"), lax.axis_index("blk_1")
     x, core = lax.axis_index("tm_0"), lax.axis_index("tm_1")
     me = y * 4 + z
@@ -126,10 +69,15 @@
         return 0
 
     lax.fori_loop(1, 16, greet, 0)
-    pl.semaphore_signal(barrier, inc=1, device_id={"tm_0": right}, device_id_type=MESH)
-    pl.semaphore_signal(barrier, inc=1, device_id={"tm_0": left}, device_id_type=MESH)
-    pl.semaphore_signal(barrier, inc=1, device_id={"tm_1": 1 - core}, device_id_type=MESH)
-    pl.semaphore_wait(barrier, 18)
+
+    def in_line(k):
+        return {"tm_0": (x + k // 2) % 4, "tm_1": (core + k) % 2}
+
+    def greet_line(k, _):
+        pl.semaphore_signal(barrier, inc=1, device_id=in_line(k), device_id_type=MESH)
+        return 0
+
+    lax.fori_loop(1, 8, greet_line, 0)
     side = ({"tm_0": right}, {"tm_0": left})
     peer = {"tm_1": 1 - core}
 
@@ -140,12 +88,12 @@
 
     def in_copy(g, k):
         ty, tz = (y + k // 4) % 4, (z + k % 4) % 4
-        return remote(spectra.at[ty * 4 + tz, g], recv.at[g, me], in_send.at[g, k],
+        return remote(spectra.at[g, ty * 4 + tz], recv.at[g, me], in_send.at[g, k],
                       in_recv.at[g, k], {"blk_0": ty, "blk_1": tz})
 
     def out_copy(g, k):
         ty, tz = (y + k // 4) % 4, (z + k % 4) % 4
-        return remote(blocks.at[g, ty * 4 + tz], out.at[me, g], out_send.at[g, k],
+        return remote(blocks.at[g, ty * 4 + tz], out.at[g, me], out_send.at[g, k],
                       out_recv.at[g, k], {"blk_0": ty, "blk_1": tz})
 
     def hours(plane, who):
@@ -316,29 +264,81 @@
             return 0
 
         lax.fori_loop(1, 16, send, 0)
-        out[pl.ds(me, 1), g] = blocks[g, pl.ds(me, 1)]
-
-    def send_in(n, _):
-        in_copy(n // 15, n % 15 + 1).start()
-        return 0
-
-    lax.fori_loop(0, GROUPS * 15, send_in, 0)
+        out[g, pl.ds(me, 1)] = blocks[g, pl.ds(me, 1)]
+
+    def sum_copy(k):
+        return remote(stage.at[0], line.at[x * 2 + core], sum_send.at[k], sum_recv.at[k], in_line(k))
+
+    def all_copy(k):
+        return remote(stage.at[1], plane.at[me], all_send.at[k], all_recv.at[k],
+                      {"blk_0": (y + k // 4) % 4, "blk_1": (z + k % 4) % 4})
+
+    def order_rows(block, odd):
+        sub = lax.broadcasted_iota(jnp.int32, (ORD, 128), 0)
+        value = jnp.zeros((ORD, 128), jnp.int32)
+        for i in range(ORD):
+            value = jnp.where(sub == i, orders[block * 32 + odd * ORD + i], value)
+        low = jnp.minimum(value, 511 - value)
+        return low + jnp.where(value == low, 0, 1024)
+
+    loads[0].wait()
+    lat, time = 32, 16
+    for q in range(8):
+        split[q * 512 : (q + 1) * 512, :] = direction[:, q * 128 : (q + 1) * 128]
+
+    def gather(t, _):
+        for q in range(8):
+            rows[pl.ds(pl.multiple_of(t * lat, lat), lat), q * 128 : (q + 1) * 128] = split[
+                pl.ds(q * 512 + t, lat, stride=time), :
+            ].astype(BF)
+        return 0
+
+    lax.fori_loop(0, time, gather, 0, unroll=2)
+    lane = lax.broadcasted_iota(jnp.int32, (4 * ORD, 128), 1)
+    scale = 1.0 / math.sqrt(512.0)
     for g in range(GROUPS):
-        recv[g, pl.ds(me, 1)] = spectra[pl.ds(me, 1), g]
+        def fill(n, _):
+            m = jnp.concatenate([order_rows(n * 4 + k, g % 2) for k in range(4)], axis=0) % 1024
+            m = m if g < 2 else 511 - m
+            cos, sin = unit_circle((m * lane) % 1024)
+            turn_c, turn_s = unit_circle((m * 128) % 1024)
+            cos, sin = cos * scale, sin * scale
+            for q in range(8):
+                both = jnp.concatenate(
+                    [v[k * ORD : (k + 1) * ORD] for k in range(4) for v in (cos, sin)], axis=0)
+                table[pl.ds(pl.multiple_of(g * 256 + n * 64, 64), 64), q * 128 : (q + 1) * 128] = (
+                    both.astype(BF))
+                cos, sin = cos * turn_c - sin * turn_s, sin * turn_c + cos * turn_s
+            return 0
+
+        lax.fori_loop(0, 4, fill, 0)
+        spectra[g] = lax.dot_general(
+            table[g * 256 : (g + 1) * 256, :], rows[...], (((1,), (1,)), ((), ())),
+            preferred_element_type=F32).astype(BF).reshape(16, 2 * ORD, 512)
+        if g == 0:
+            pl.semaphore_wait(barrier, 22)
+
+        def send_in(k, _):
+            in_copy(g, k).start()
+            return 0
+
+        lax.fori_loop(1, 16, send_in, 0)
+        recv[g, pl.ds(me, 1)] = spectra[g, pl.ds(me, 1)]
     perm[...] = lane_swap()
+    arrive(0)
     degree = (x * 2 + core) * 64 + lax.broadcasted_iota(jnp.int32, (64, 512), 0)
-
-    def mask(k, _):
-        both = (legendre[k].astype(F32), legendre[16 + k].astype(F32))
-        for h in range(2):
-            entry = jnp.concatenate([orders[pl.ds(me * 32 + h * 16 + k, 1), :]] * 4, axis=1)
-            entry = jnp.broadcast_to(entry, (64, 512))
-            row = jnp.where(entry >= 1024, both[1 - h], both[h])
-            leg[h * 16 + k] = jnp.where(degree >= entry % 1024, row, 0.0).astype(BF)
-        return 0
-
-    lax.fori_loop(0, 16, mask, 0)
-    arrive(0)
+    loads[1].wait()
+    loads[2].wait()
+    for odd in range(2):
+        entry_rows = order_rows(me, odd)
+        for k in range(ORD):
+            n = odd * ORD + k
+            first, second = legendre[n].astype(F32), legendre[16 + n].astype(F32)
+            entry = jnp.broadcast_to(
+                jnp.concatenate([entry_rows[k : k + 1, :]] * 4, axis=1), (64, 512))
+            swap, low = entry >= 1024, entry % 1024
+            leg[n] = jnp.where(degree >= low, jnp.where(swap, second, first), 0.0).astype(BF)
+            leg[16 + n] = jnp.where(degree >= 511 - low, jnp.where(swap, first, second), 0.0).astype(BF)
     arrive(1)
     forward(0)
     arrive(2)
@@ -365,7 +365,83 @@
     depart(1)
     add_far(3)
     depart(2)
+
+    def arrived(g):
+        def wait(k, _):
+            out_copy(g, k).wait_recv()
+            return 0
+
+        lax.fori_loop(1, 16, wait, 0)
+
+    def transform(first, count, n):
+        cols = pl.ds(pl.multiple_of(n * 128, 128), 128)
+        value = out[first : first + count, :, :, cols].reshape(count * 256, 128)
+        return lax.dot_general(
+            value, table[first * 256 : (first + count) * 256, :], (((0,), (0,)), ((), ())),
+            preferred_element_type=F32)
+
+    arrived(0)
+    arrived(1)
+
+    def partial(n, _):
+        synth[pl.ds(pl.multiple_of(n * 128, 128), 128), :] = transform(0, 2, n)
+        return 0
+
+    lax.fori_loop(0, 4, partial, 0)
     depart(3)
+    arrived(2)
+
+    def partial2(n, _):
+        synth[pl.ds(pl.multiple_of(n * 128, 128), 128), :] += transform(2, 1, n)
+        return 0
+
+    lax.fori_loop(0, 4, partial2, 0)
+    loads[3].wait()
+    loads[4].wait()
+    arrived(3)
+
+    def synthesis(n, _):
+        block = synth[pl.ds(pl.multiple_of(n * 128, 128), 128), :] + transform(3, 1, n)
+        for t in range(4):
+            for q in range(8):
+                split[pl.ds(q * 512 + n * 4 + t, 32, stride=16), :] = (
+                    block[t * 32 : (t + 1) * 32, q * 128 : (q + 1) * 128])
+        return 0
+
+    lax.fori_loop(0, 4, synthesis, 0)
+
+    def combine(n, totals):
+        r8 = pl.ds(pl.multiple_of(n * 8, 8), 8)
+        nn, dp, rp, pp = totals
+        for q in range(8):
+            cols = slice(q * 128, (q + 1) * 128)
+            d, r = direction[r8, cols], residual[r8, cols]
+            p = split[pl.ds(pl.multiple_of(q * 512 + n * 8, 8), 8), :] + noise[r8, cols] * d
+            product[r8, cols] = p
+            nn, dp, rp, pp = nn + r * r, dp + d * p, rp + r * p, pp + p * p
+        return nn, dp, rp, pp
+
+    zero = jnp.zeros((8, 128), F32)
+    totals = lax.fori_loop(0, 64, combine, (zero, zero, zero, zero), unroll=2)
+    for k in range(4):
+        stage[0, 2 * k : 2 * k + 2, :] = jnp.broadcast_to(
+            jnp.sum(totals[k], axis=0, keepdims=True), (2, 128))
+    for k in range(1, 8):
+        sum_copy(k).start()
+    line[pl.ds(x * 2 + core, 1)] = stage[0:1]
+    for k in range(1, 8):
+        sum_copy(k).wait_recv()
+    stage[1] = jnp.sum(line[...], axis=0)
+    for k in range(1, 16):
+        all_copy(k).start()
+    plane[pl.ds(me, 1)] = stage[1:2]
+    for k in range(1, 16):
+        all_copy(k).wait_recv()
+    sums[...] = jnp.sum(plane[...], axis=0)
+    for k in range(1, 8):
+        sum_copy(k).wait_send()
+    for k in range(1, 16):
+        all_copy(k).wait_send()
     for g in range(GROUPS):
         for slot in range(5):
             dup_copy(g, slot).wait_send()
@@ -379,22 +455,31 @@
 
     def finish(n, _):
         in_copy(n // 15, n % 15 + 1).wait_send()
-        out_copy(n // 15, n % 15 + 1).wait_recv()
         out_copy(n // 15, n % 15 + 1).wait_send()
         return 0
 
     lax.fori_loop(0, GROUPS * 15, finish, 0)
 
 
-def core_stage(spectra, orders, legendre, temporal):
+def step_stage(orders, direction, residual, noise, legendre, temporal):
     dma = pltpu.SemaphoreType.DMA
     two, four, five, blk = dma((GROUPS, 2)), dma((GROUPS, 4)), dma((GROUPS, 5)), dma((GROUPS, 16))
+    grid = pltpu.VMEM((512, 1024), F32)
+    hbm = pl.BlockSpec(memory_space=pl.ANY)
     return pl.pallas_call(
-        core_kernel,
-        out_shape=jax.ShapeDtypeStruct((16, GROUPS, 2 * ORD, 512), BF),
-        in_specs=[VM] * 4,
-        out_specs=VM,
+        step_kernel,
+        out_shape=(jax.ShapeDtypeStruct((512, 1024), F32), jax.ShapeDtypeStruct((8, 128), F32)),
+        in_specs=[pl.BlockSpec(memory_space=pltpu.SMEM)] + [hbm] * 5,
+        out_specs=(VM, VM),
         scratch_shapes=[
+            grid, grid, grid,
+            pltpu.VMEM((32, 64, 512), BF),
+            pltpu.VMEM((64, 128, 128), F32),
+            dma((5,)),
+            pltpu.VMEM((4096, 128), F32),
+            pltpu.VMEM((512, 1024), BF),
+            pltpu.VMEM((1024, 1024), BF),
+            pltpu.VMEM((GROUPS, 16, 2 * ORD, 512), BF),
             pltpu.VMEM((32, 2, 128, 512), BF),
             pltpu.VMEM((32, 2, 128, 512), BF),
             pltpu.VMEM((32, 64, 512), BF),
@@ -407,114 +492,18 @@
             pltpu.VMEM((GROUPS, 4, ORD, 2, 16, 512), BF),
             pltpu.VMEM((GROUPS, 2, ORD // 2, 2, 16, 512), BF),
             pltpu.VMEM((GROUPS, 2, ORD, 2, 16, 512), BF),
-            blk, blk, two, two, five, two, two, five, four, four, two, two, two, two, blk, blk,
-        ],
-        compiler_params=pltpu.CompilerParams(
-            collective_id=0, has_side_effects=True, vmem_limit_bytes=48 * 1024 * 1024),
-        name="core_stage",
-    )(spectra, orders, legendre, temporal)
-
-
-def product_kernel(entries, table, residual, direction, noise, product, sums, split, stage, line,
-                   plane, line_send, line_recv, plane_send, plane_recv):
-    y, z = lax.axis_index("blk_0"), lax.axis_index("blk_1")
-    x, core = lax.axis_index("tm_0"), lax.axis_index("tm_1")
-    row, col = y * 4 + z, x * 2 + core
-
-    def in_line(k):
-        return {"tm_0": (x + k // 2) % 4, "tm_1": (core + k) % 2}
-
-    def in_plane(k):
-        return {"blk_0": (y + k // 4) % 4, "blk_1": (z + k % 4) % 4}
-
-    barrier = pltpu.get_barrier_semaphore()
-
-    def greet_line(k, _):
-        pl.semaphore_signal(barrier, inc=1, device_id=in_line(k), device_id_type=MESH)
-        return 0
-
-    def greet_plane(k, _):
-        pl.semaphore_signal(barrier, inc=1, device_id=in_plane(k), device_id_type=MESH)
-        return 0
-
-    lax.fori_loop(1, 8, greet_line, 0)
-    lax.fori_loop(1, 16, greet_plane, 0)
-
-    def synthesis(n, _):
-        cols = entries[:, pl.ds(pl.multiple_of(n * 128, 128), 128)]
-        block = lax.dot_general(cols, table[...], (((0,), (0,)), ((), ())), preferred_element_type=F32)
-        for t in range(4):
-            for q in range(8):
-                split[pl.ds(q * 512 + n * 4 + t, 32, stride=16), :] = (
-                    block[t * 32 : (t + 1) * 32, q * 128 : (q + 1) * 128])
-        return 0
-
-    lax.fori_loop(0, 4, synthesis, 0)
-
-    def combine(n, totals):
-        rows = pl.ds(pl.multiple_of(n * 8, 8), 8)
-        nn, dp, rp, pp = totals
-        for q in range(8):
-            cols = slice(q * 128, (q + 1) * 128)
-            d, r = direction[rows, cols], residual[rows, cols]
-            p = split[pl.ds(pl.multiple_of(q * 512 + n * 8, 8), 8), :] + noise[rows, cols] * d
-            product[rows, cols] = p
-            nn, dp, rp, pp = nn + r * r, dp + d * p, rp + r * p, pp + p * p
-        return nn, dp, rp, pp
-
-    zero = jnp.zeros((8, 128), F32)
-    totals = lax.fori_loop(0, 64, combine, (zero, zero, zero, zero))
-    for k in range(4):
-        stage[0, 2 * k : 2 * k + 2, :] = jnp.broadcast_to(
-            jnp.sum(totals[k], axis=0, keepdims=True), (2, 128))
-    pl.semaphore_wait(barrier, 22)
-
-    def line_copy(k):
-        return pltpu.make_async_remote_copy(
-            src_ref=stage.at[0], dst_ref=line.at[col], send_sem=line_send.at[k],
-            recv_sem=line_recv.at[k], device_id=in_line(k), device_id_type=MESH)
-
-    def plane_copy(k):
-        return pltpu.make_async_remote_copy(
-            src_ref=stage.at[1], dst_ref=plane.at[row], send_sem=plane_send.at[k],
-            recv_sem=plane_recv.at[k], device_id=in_plane(k), device_id_type=MESH)
-
-    for k in range(1, 8):
-        line_copy(k).start()
-    line[pl.ds(col, 1)] = stage[0:1]
-    for k in range(1, 8):
-        line_copy(k).wait_recv()
-    stage[1] = jnp.sum(line[...], axis=0)
-    for k in range(1, 16):
-        plane_copy(k).start()
-    plane[pl.ds(row, 1)] = stage[1:2]
-    for k in range(1, 16):
-        plane_copy(k).wait_recv()
-    sums[...] = jnp.sum(plane[...], axis=0)
-    for k in range(1, 8):
-        line_copy(k).wait_send()
-    for k in range(1, 16):
-        plane_copy(k).wait_send()
-
-
-def product_sums(entries, table, residual, direction, noise):
-    dma = pltpu.SemaphoreType.DMA
-    return pl.pallas_call(
-        product_kernel,
-        out_shape=(jax.ShapeDtypeStruct((512, 1024), F32), jax.ShapeDtypeStruct((8, 128), F32)),
-        in_specs=[VM] * 5,
-        out_specs=(VM, VM),
-        scratch_shapes=[
-            pltpu.VMEM((4096, 128), F32),
+            pltpu.VMEM((GROUPS, 16, 2 * ORD, 512), BF),
+            grid,
             pltpu.VMEM((2, 8, 128), F32),
             pltpu.VMEM((8, 8, 128), F32),
             pltpu.VMEM((16, 8, 128), F32),
+            blk, blk, two, two, five, two, two, five, four, four, two, two, two, two, blk, blk,
             dma((8,)), dma((8,)), dma((16,)), dma((16,)),
         ],
         compiler_params=pltpu.CompilerParams(
-            collective_id=2, has_side_effects=True, vmem_limit_bytes=48 * 1024 * 1024),
-        name="product_sums",
-    )(entries, table, residual, direction, noise)
+            collective_id=0, has_side_effects=True, vmem_limit_bytes=54 * 1024 * 1024),
+        name="step_stage",
+    )(orders, direction, residual, noise, legendre, temporal)
 
 
 def update_kernel(sums, solution, residual, direction, product, solution_new, residual_new,
@@ -570,10 +559,8 @@
 def body(solution, residual, direction, noise_var, legendre, temporal, order_table):
     shape = direction.shape
     flat = lambda v: v.reshape(512, 1024)
-    orders = order_groups(order_table)
-    table, spectra = table_dft(orders, flat(direction))
-    entries = core_stage(spectra, orders, legendre, temporal).reshape(1024, 512)
-    product, sums = product_sums(entries, table, flat(residual), flat(direction), flat(noise_var))
+    product, sums = step_stage(
+        order_table, flat(direction), flat(residual), flat(noise_var), legendre, temporal)
     outs = update(sums, flat(solution), flat(residual), flat(direction), product)
     return tuple(o.reshape(shape) for o in outs)
 

time: 125 us -> 117 us (0.936)
  Pallas kernels: 122 us -> 114 us
    pallas_call x3 -> x1, Pallas kernels: 119 us -> 111 us  [step_stage(): pl.pallas_call(step_kernel, out_shape=(jax.ShapeDtypeStruct((512, 1024),...]
where the time goes in v2:
time: 117 us
  Pallas kernels  114 us (97%)
  local copies, waits for them, and re-layouts  2.27 us (2%)
    pallas_call x1, Pallas kernels, step_stage(): pl.pallas_call(step_kernel, out_shape=(jax.ShapeDtypeStruct((512, 1024),...  111 us
    pallas_call x1, Pallas kernels, update(): pl.pallas_call(update_kernel, out_shape=(shape, shape, shape), in_specs=[...  3 us

profile of v2, /device:TPU:1, one launch (start us, length us, event | category | flops | bytes accessed | tf_op | source)
XLA Modules:
  0.0 117.3 jit_solution(6899304571255041570)
XLA Ops:
  0.6 0.0 copy-start
  0.6 0.0 copy-start.1
  0.7 0.0 copy-start.2
  0.7 111.3 %step_stage.1 = (f32[512,1024]{1,0:T(8,128)}, f32[8,128]{1,0:T(8,128)}) custom-call(s32[512]{0:T(512)} %orders.1, f32[512,1024]{1,0:T(8,128)} %bitcast.7, f32[512,1024]{1,0:T(8,128)} %bitcast.9, f32[512,1024]{1,0:T(8,128)} %bitcast.12, bf16[32,64,512]{2,1,0:T(8,128)(2,1)} %legendre_in.1, f32[64,128,128]{2,1,0:T(8,128)} %temporal_in.1), custom_call_target="tpu_custom_call" | custom-call | tf_op jit(solution)/shard_map/step_stage/pallas_call | solution.py:469
  112.0 0.0 copy-done
  112.0 0.0 copy-done.1
  112.0 0.0 copy-done.2
  112.0 0.0 copy-start.3
  112.0 1.6 %copy-done.3 = f32[512,1024]{1,0:T(8,128)S(1)} copy-done((f32[512,1024]{1,0:T(8,128)S(1)}, f32[512,1024]{1,0:T(8,128)}, u32[]{:S(2)}) %copy-start.3) | copy-done | bytes 2097176
  113.6 0.0 copy-start.4
  113.6 0.7 copy-done.4
  114.3 3.0 %update.1 = (f32[512,1024]{1,0:T(8,128)}, f32[512,1024]{1,0:T(8,128)}, f32[512,1024]{1,0:T(8,128)}) custom-call(f32[8,128]{1,0:T(8,128)S(1)} %copy-done.4, f32[512,1024]{1,0:T(8,128)S(1)} %bitcast.11, f32[512,1024]{1,0:T(8,128)S(1)} %bitcast.10, f32[512,1024]{1,0:T(8,128)S(1)} %bitcast.8, f32[512,1024]{1,0:T(8,128)S(1)} %copy-done.3), custom_call_target="tpu_custom_call" | custom-call | tf_op jit(solution)/shard_map/update/pallas_call | solution.py:548
Async XLA Ops:
  0.6 111.4 %copy-start = (f32[32,16,1024]{2,1,0:T(8,128)S(1)}, f32[32,16,1024]{2,1,0:T(8,128)}, u32[]{:S(2)}) copy-start(f32[32,16,1024]{2,1,0:T(8,128)} %param.9) | copy-start | bytes 6291460
  0.6 111.4 %copy-start.1 = (f32[32,16,1024]{2,1,0:T(8,128)S(1)}, f32[32,16,1024]{2,1,0:T(8,128)}, u32[]{:S(2)}) copy-start(f32[32,16,1024]{2,1,0:T(8,128)} %param.8) | copy-start | bytes 6291460
  0.7 111.4 %copy-start.2 = (f32[32,16,1024]{2,1,0:T(8,128)S(1)}, f32[32,16,1024]{2,1,0:T(8,128)}, u32[]{:S(2)}) copy-start(f32[32,16,1024]{2,1,0:T(8,128)} %param.7) | copy-start | bytes 6291460
  112.0 1.6 %copy-start.3 = (f32[512,1024]{1,0:T(8,128)S(1)}, f32[512,1024]{1,0:T(8,128)}, u32[]{:S(2)}) copy-start(f32[512,1024]{1,0:T(8,128)} %get-tuple-element.9.product) | copy-start | bytes 6291460
  113.6 0.7 copy-start.4

commit v3 on v2

--- a/solution.py
+++ b/solution.py
@@ -16,6 +16,7 @@
 MESH = pl.DeviceIdType.MESH
 GROUPS = 4
 ORD = 8
+FIRST = (4, 5, 6, 0)
 VM = pl.BlockSpec(memory_space=pltpu.VMEM)
 
 
@@ -40,17 +41,17 @@
     return (col == moved).astype(F32).astype(BF)
 
 
-def step_kernel(orders, direction_in, residual_in, noise_in, legendre_in, temporal_in, product, sums,
-                direction, residual, noise, legendre, temporal, load, split, rows, table, spectra,
-                full, part, leg, recv, blocks, mid, perm, coef, mixed, acc, far_in, fin_in, out, synth,
-                stage, line, plane, in_send, in_recv, own_send, fwd_send, dup_send,
+def step_kernel(orders, direction_in, residual_in, solution_in, noise_in, legendre_in, temporal_in,
+                product, sums, direction, residual, solution, noise, legendre, temporal, load, split,
+                rows, table, spectra, ring, full, part, leg, recv, blocks, mid, perm, coef, mixed, acc,
+                far_in, fin_in, last_far, last_fin, last, out, synth, stage, line, plane, in_send, in_recv, own_send, fwd_send, dup_send,
                 own_recv, fwd_recv, dup_recv, pair_send, pair_recv, far_send, far_recv, line_send,
                 line_recv, out_send, out_recv, sum_send, sum_recv, all_send, all_recv):
     loads = [
         pltpu.make_async_copy(src, dst, load.at[n])
         for n, (src, dst) in enumerate((
             (direction_in, direction), (legendre_in, legendre), (temporal_in, temporal),
-            (residual_in, residual), (noise_in, noise)))
+            (residual_in, residual), (noise_in, noise), (solution_in, solution)))
     ]
     for copy in loads:
         copy.start()
@@ -91,6 +92,37 @@
         return remote(spectra.at[g, ty * 4 + tz], recv.at[g, me], in_send.at[g, k],
                       in_recv.at[g, k], {"blk_0": ty, "blk_1": tz})
 
+    def in_first(slot, k):
+        ty, tz = (y + k // 4) % 4, (z + k % 4) % 4
+        dest = ty * 4 + tz
+        src = spectra.at[0, dest] if slot == 3 else ring.at[slot, dest]
+        return remote(src, recv.at[FIRST[slot], me], in_send.at[FIRST[slot], k],
+                      in_recv.at[FIRST[slot], k], {"blk_0": ty, "blk_1": tz})
+
+    def ring_copy(way):
+        return remote(spectra.at[0], ring.at[way], own_send.at[0, way], own_recv.at[0, way], side[way])
+
+    def ring_forward(way):
+        return remote(ring.at[way, pl.ds(way * 8, 8)], ring.at[2, pl.ds(way * 8, 8)],
+                      fwd_send.at[0, way], fwd_recv.at[0, way], side[way])
+
+    def dup_first(slot):
+        ref = piece(0, (left, right, far, x)[slot], 0, ORD)
+        return remote(ref, ref, dup_send.at[0, slot], dup_recv.at[0, slot], peer)
+
+    def out_last(n, k):
+        ty, tz = (y + k // 4) % 4, (z + k % 4) % 4
+        return remote(blocks.at[3 + n, ty * 4 + tz], last.at[n, me], out_send.at[3 + n, k],
+                      out_recv.at[3 + n, k], {"blk_0": ty, "blk_1": tz})
+
+    def last_far_copy(way):
+        return remote(last.at[0, pl.ds(way * 8, 8)], last_far.at[way], far_send.at[3, way],
+                      far_recv.at[3, way], side[way])
+
+    def last_line_copy(way):
+        return remote(last.at[1 + way], last_fin.at[way], line_send.at[3, way],
+                      line_recv.at[3, way], side[way])
+
     def out_copy(g, k):
         ty, tz = (y + k // 4) % 4, (z + k % 4) % 4
         return remote(blocks.at[g, ty * 4 + tz], out.at[g, me], out_send.at[g, k],
@@ -130,32 +162,65 @@
         return remote(acc.at[g, 1 + way], fin_in.at[g, way], line_send.at[g, way],
                       line_recv.at[g, way], side[way])
 
+    def regroup_in(n, g, plane_of):
+        blocks_in = []
+        for sq in range(4):
+            for tq in range(4):
+                blocks_in.append(jnp.concatenate(
+                    [recv[n, sq * 4 + s, :, tq * 128 : (tq + 1) * 128] for s in range(4)], axis=1))
+        moved = jnp.dot(jnp.concatenate(blocks_in, axis=0), perm[...], preferred_element_type=F32)
+        for sq in range(4):
+            for tq in range(4):
+                n0 = (sq * 4 + tq) * 16
+                for t in range(4):
+                    m = sq * 256 + (tq * 4 + t) * 16
+                    mid[m : m + 16, :] = moved[n0 : n0 + 16, t * 128 : (t + 1) * 128]
+        for c in range(2):
+            for i in range(ORD):
+                for sq in range(4):
+                    full[g * ORD + i, c, hours(plane_of, core), sq * 128 : (sq + 1) * 128] = (
+                        mid[pl.ds(sq * 256 + c * ORD + i, 16, stride=16), :].astype(BF))
+
     def arrive(g):
         def wait(k, _):
             in_copy(g, k).wait_recv()
             return 0
 
         lax.fori_loop(1, 16, wait, 0)
-        rows = []
-        for sq in range(4):
-            for tq in range(4):
-                rows.append(jnp.concatenate(
-                    [recv[g, sq * 4 + s, :, tq * 128 : (tq + 1) * 128] for s in range(4)], axis=1))
-        moved = jnp.dot(jnp.concatenate(rows, axis=0), perm[...], preferred_element_type=F32)
-        for sq in range(4):
-            for tq in range(4):
-                n = (sq * 4 + tq) * 16
-                for t in range(4):
-                    m = sq * 256 + (tq * 4 + t) * 16
-                    mid[m : m + 16, :] = moved[n : n + 16, t * 128 : (t + 1) * 128]
-        for c in range(2):
-            for i in range(ORD):
-                for sq in range(4):
-                    full[g * ORD + i, c, hours(x, core), sq * 128 : (sq + 1) * 128] = (
-                        mid[pl.ds(sq * 256 + c * ORD + i, 16, stride=16), :].astype(BF))
+        regroup_in(g, g, x)
         own_copy(g, 0).start()
         own_copy(g, 1).start()
         dup_copy(g, 0).start()
+
+    def send_first(slot):
+        def send(k, _):
+            in_first(slot, k).start()
+            return 0
+
+        lax.fori_loop(1, 16, send, 0)
+        src = spectra if slot == 3 else ring
+        recv[FIRST[slot], pl.ds(me, 1)] = src[0 if slot == 3 else slot, pl.ds(me, 1)]
+
+    def arrive_first(slot):
+        def wait(k, _):
+            in_first(slot, k).wait_recv()
+            return 0
+
+        lax.fori_loop(1, 16, wait, 0)
+        regroup_in(FIRST[slot], 0, (left, right, far, x)[slot])
+        dup_first(slot).start()
+
+    def forward_first():
+        for way in range(2):
+            ring_copy(way).wait_recv()
+            ring_forward(way).start()
+        for way in range(2):
+            send_first(way)
+
+    def far_first():
+        for way in range(2):
+            ring_forward(way).wait_recv()
+        send_first(2)
 
     def forward(g):
         for way in range(2):
@@ -169,8 +234,12 @@
             dup_copy(g, 3 + way).start()
 
     def middle(g):
-        for slot in range(5):
-            dup_copy(g, slot).wait_recv()
+        if g == 0:
+            for slot in range(4):
+                dup_first(slot).wait_recv()
+        else:
+            for slot in range(5):
+                dup_copy(g, slot).wait_recv()
 
         def analyse(i, _):
             value = lax.dot_general(
@@ -217,7 +286,16 @@
                 return 0
 
             lax.fori_loop(0, ORD, step, 0)
-            if n == 0:
+            if g == GROUPS - 1:
+                regroup_out(3 + n, lambda i, c: acc[g, n, i, c].astype(F32))
+
+                def send(k, _):
+                    out_last(n, k).start()
+                    return 0
+
+                lax.fori_loop(1, 16, send, 0)
+                last[n, pl.ds(me, 1)] = blocks[3 + n, pl.ds(me, 1)]
+            elif n == 0:
                 far_copy(g, 0).start()
                 far_copy(g, 1).start()
 
@@ -234,30 +312,33 @@
             lax.fori_loop(0, half, step, 0)
             line_copy(g, way).start()
 
+    def regroup_out(n, value):
+        for i in range(ORD):
+            for c in range(2):
+                total = value(i, c)
+                for sq in range(4):
+                    mid[pl.ds(sq * 256 + c * ORD + i, 16, stride=16), :] = (
+                        total[:, sq * 128 : (sq + 1) * 128])
+        rows_out = []
+        for sq in range(4):
+            for tq in range(4):
+                m = sq * 256 + tq * 64
+                rows_out.append(jnp.concatenate(
+                    [mid[m + t * 16 : m + (t + 1) * 16, :].astype(BF) for t in range(4)], axis=1))
+        moved = jnp.dot(
+            jnp.concatenate(rows_out, axis=0), perm[...], preferred_element_type=F32).astype(BF)
+        for sq in range(4):
+            for tq in range(4):
+                n0 = (sq * 4 + tq) * 16
+                for s in range(4):
+                    blocks[n, sq * 4 + s, :, tq * 128 : (tq + 1) * 128] = (
+                        moved[n0 : n0 + 16, s * 128 : (s + 1) * 128])
+
     def depart(g):
         line_copy(g, 0).wait_recv()
         line_copy(g, 1).wait_recv()
-        for i in range(ORD):
-            for c in range(2):
-                total = (acc[g, 3, i, c].astype(F32) + fin_in[g, 0, i, c].astype(F32)
-                         + fin_in[g, 1, i, c].astype(F32))
-                for sq in range(4):
-                    mid[pl.ds(sq * 256 + c * ORD + i, 16, stride=16), :] = (
-                        total[:, sq * 128 : (sq + 1) * 128])
-        rows = []
-        for sq in range(4):
-            for tq in range(4):
-                m = sq * 256 + tq * 64
-                rows.append(jnp.concatenate(
-                    [mid[m + t * 16 : m + (t + 1) * 16, :].astype(BF) for t in range(4)], axis=1))
-        moved = jnp.dot(
-            jnp.concatenate(rows, axis=0), perm[...], preferred_element_type=F32).astype(BF)
-        for sq in range(4):
-            for tq in range(4):
-                n = (sq * 4 + tq) * 16
-                for s in range(4):
-                    blocks[g, sq * 4 + s, :, tq * 128 : (tq + 1) * 128] = (
-                        moved[n : n + 16, s * 128 : (s + 1) * 128])
+        regroup_out(g, lambda i, c: acc[g, 3, i, c].astype(F32) + fin_in[g, 0, i, c].astype(F32)
+                    + fin_in[g, 1, i, c].astype(F32))
 
         def send(k, _):
             out_copy(g, k).start()
@@ -265,6 +346,25 @@
 
         lax.fori_loop(1, 16, send, 0)
         out[g, pl.ds(me, 1)] = blocks[g, pl.ds(me, 1)]
+
+    def last_arrived(n):
+        def wait(k, _):
+            out_last(n, k).wait_recv()
+            return 0
+
+        lax.fori_loop(1, 16, wait, 0)
+
+    def last_add(way):
+        last_arrived(1 + way)
+        last_far_copy(way).wait_recv()
+
+        def step(j, _):
+            last[1 + way, way * 8 + j] = (
+                last[1 + way, way * 8 + j].astype(F32) + last_far[way, j].astype(F32)).astype(BF)
+            return 0
+
+        lax.fori_loop(0, 8, step, 0)
+        last_line_copy(way).start()
 
     def sum_copy(k):
         return remote(stage.at[0], line.at[x * 2 + core], sum_send.at[k], sum_recv.at[k], in_line(k))
@@ -318,14 +418,22 @@
         if g == 0:
             pl.semaphore_wait(barrier, 22)
 
+            ring_copy(0).start()
+            ring_copy(1).start()
+            continue
+
         def send_in(k, _):
             in_copy(g, k).start()
             return 0
 
         lax.fori_loop(1, 16, send_in, 0)
         recv[g, pl.ds(me, 1)] = spectra[g, pl.ds(me, 1)]
+        if g == 1:
+            send_first(3)
     perm[...] = lane_swap()
-    arrive(0)
+    arrive(1)
+    forward_first()
+    arrive(2)
     degree = (x * 2 + core) * 64 + lax.broadcasted_iota(jnp.int32, (64, 512), 0)
     loads[1].wait()
     loads[2].wait()
@@ -339,32 +447,34 @@
             swap, low = entry >= 1024, entry % 1024
             leg[n] = jnp.where(degree >= low, jnp.where(swap, second, first), 0.0).astype(BF)
             leg[16 + n] = jnp.where(degree >= 511 - low, jnp.where(swap, first, second), 0.0).astype(BF)
-    arrive(1)
-    forward(0)
-    arrive(2)
+    far_first()
+    arrive_first(3)
     forward(1)
-    forward_far(0)
     arrive(3)
+    arrive_first(0)
+    arrive_first(1)
+    arrive_first(2)
+    forward_far(1)
     middle(0)
     forward(2)
-    forward_far(1)
     add_pair(0)
     middle(1)
     forward(3)
+    forward_far(2)
     add_pair(1)
-    forward_far(2)
     middle(2)
+    forward_far(3)
     add_far(0)
     add_pair(2)
-    forward_far(3)
     middle(3)
     add_far(1)
     add_pair(3)
     depart(0)
     add_far(2)
+    last_arrived(0)
+    last_far_copy(0).start()
+    last_far_copy(1).start()
     depart(1)
-    add_far(3)
-    depart(2)
 
     def arrived(g):
         def wait(k, _):
@@ -380,6 +490,9 @@
             value, table[first * 256 : (first + count) * 256, :], (((0,), (0,)), ((), ())),
             preferred_element_type=F32)
 
+    last_add(0)
+    last_add(1)
+    depart(2)
     arrived(0)
     arrived(1)
 
@@ -388,7 +501,9 @@
         return 0
 
     lax.fori_loop(0, 4, partial, 0)
-    depart(3)
+    for n in range(3, 6):
+        loads[n].wait()
+    last_arrived(3)
     arrived(2)
 
     def partial2(n, _):
@@ -396,9 +511,15 @@
         return 0
 
     lax.fori_loop(0, 4, partial2, 0)
-    loads[3].wait()
-    loads[4].wait()
-    arrived(3)
+    for way in range(2):
+        last_line_copy(way).wait_recv()
+
+    def total(j, _):
+        out[3, j] = (last[3, j].astype(F32) + last_fin[0, j].astype(F32)
+                     + last_fin[1, j].astype(F32)).astype(BF)
+        return 0
+
+    lax.fori_loop(0, 16, total, 0)
 
     def synthesis(n, _):
         block = synth[pl.ds(pl.multiple_of(n * 128, 128), 128), :] + transform(3, 1, n)
@@ -443,55 +564,72 @@
     for k in range(1, 16):
         all_copy(k).wait_send()
     for g in range(GROUPS):
-        for slot in range(5):
-            dup_copy(g, slot).wait_send()
         for n in range(4):
             pair_copy(g, n).wait_send()
         for way in range(2):
-            own_copy(g, way).wait_send()
-            fwd_copy(g, way).wait_send()
-            far_copy(g, way).wait_send()
-            line_copy(g, way).wait_send()
-
-    def finish(n, _):
-        in_copy(n // 15, n % 15 + 1).wait_send()
-        out_copy(n // 15, n % 15 + 1).wait_send()
-        return 0
-
-    lax.fori_loop(0, GROUPS * 15, finish, 0)
-
-
-def step_stage(orders, direction, residual, noise, legendre, temporal):
+            if g == 0:
+                ring_copy(way).wait_send()
+                ring_forward(way).wait_send()
+            else:
+                own_copy(g, way).wait_send()
+                fwd_copy(g, way).wait_send()
+            if g == GROUPS - 1:
+                last_far_copy(way).wait_send()
+                last_line_copy(way).wait_send()
+            else:
+                far_copy(g, way).wait_send()
+                line_copy(g, way).wait_send()
+        for slot in range(4 if g == 0 else 5):
+            (dup_first(slot) if g == 0 else dup_copy(g, slot)).wait_send()
+
+    def finish(k, _):
+        for g in range(1, GROUPS):
+            in_copy(g, k).wait_send()
+            out_copy(g - 1, k).wait_send()
+        for n in range(4):
+            in_first(n, k).wait_send()
+            out_last(n, k).wait_send()
+        return 0
+
+    lax.fori_loop(1, 16, finish, 0)
+
+
+def step_stage(orders, direction, residual, solution, noise, legendre, temporal):
     dma = pltpu.SemaphoreType.DMA
-    two, four, five, blk = dma((GROUPS, 2)), dma((GROUPS, 4)), dma((GROUPS, 5)), dma((GROUPS, 16))
+    two, four, five, blk = dma((GROUPS, 2)), dma((GROUPS, 4)), dma((GROUPS, 5)), dma((GROUPS + 3, 16))
     grid = pltpu.VMEM((512, 1024), F32)
     hbm = pl.BlockSpec(memory_space=pl.ANY)
+    shape = jax.ShapeDtypeStruct((512, 1024), F32)
     return pl.pallas_call(
         step_kernel,
-        out_shape=(jax.ShapeDtypeStruct((512, 1024), F32), jax.ShapeDtypeStruct((8, 128), F32)),
-        in_specs=[pl.BlockSpec(memory_space=pltpu.SMEM)] + [hbm] * 5,
-        out_specs=(VM, VM),
+        out_shape=(shape, jax.ShapeDtypeStruct((8, 128), F32), shape, shape, shape),
+        in_specs=[pl.BlockSpec(memory_space=pltpu.SMEM)] + [hbm] * 6,
+        out_specs=(VM,) * 5,
         scratch_shapes=[
-            grid, grid, grid,
+            grid,
             pltpu.VMEM((32, 64, 512), BF),
             pltpu.VMEM((64, 128, 128), F32),
-            dma((5,)),
+            dma((6,)),
             pltpu.VMEM((4096, 128), F32),
             pltpu.VMEM((512, 1024), BF),
             pltpu.VMEM((1024, 1024), BF),
             pltpu.VMEM((GROUPS, 16, 2 * ORD, 512), BF),
+            pltpu.VMEM((3, 16, 2 * ORD, 512), BF),
             pltpu.VMEM((32, 2, 128, 512), BF),
             pltpu.VMEM((32, 2, 128, 512), BF),
             pltpu.VMEM((32, 64, 512), BF),
-            pltpu.VMEM((GROUPS, 16, 2 * ORD, 512), BF),
-            pltpu.VMEM((GROUPS, 16, 2 * ORD, 512), BF),
+            pltpu.VMEM((GROUPS + 3, 16, 2 * ORD, 512), BF),
+            pltpu.VMEM((GROUPS + 3, 16, 2 * ORD, 512), BF),
             pltpu.VMEM((1024, 128), F32),
             pltpu.VMEM((512, 512), BF),
             pltpu.VMEM((2 * ORD * 64, 128), F32),
             pltpu.VMEM((2 * ORD * 64, 128), F32),
             pltpu.VMEM((GROUPS, 4, ORD, 2, 16, 512), BF),
-            pltpu.VMEM((GROUPS, 2, ORD // 2, 2, 16, 512), BF),
-            pltpu.VMEM((GROUPS, 2, ORD, 2, 16, 512), BF),
+            pltpu.VMEM((3, 2, ORD // 2, 2, 16, 512), BF),
+            pltpu.VMEM((3, 2, ORD, 2, 16, 512), BF),
+            pltpu.VMEM((2, 8, 2 * ORD, 512), BF),
+            pltpu.VMEM((2, 16, 2 * ORD, 512), BF),
+            pltpu.VMEM((4, 16, 2 * ORD, 512), BF),
             pltpu.VMEM((GROUPS, 16, 2 * ORD, 512), BF),
             grid,
             pltpu.VMEM((2, 8, 128), F32),
@@ -501,9 +639,9 @@
             dma((8,)), dma((8,)), dma((16,)), dma((16,)),
         ],
         compiler_params=pltpu.CompilerParams(
-            collective_id=0, has_side_effects=True, vmem_limit_bytes=54 * 1024 * 1024),
+            collective_id=0, has_side_effects=True, vmem_limit_bytes=58 * 1024 * 1024),
         name="step_stage",
-    )(orders, direction, residual, noise, legendre, temporal)
+    )(orders, direction, residual, solution, noise, legendre, temporal)
 
 
 def update_kernel(sums, solution, residual, direction, product, solution_new, residual_new,
@@ -559,9 +697,10 @@
 def body(solution, residual, direction, noise_var, legendre, temporal, order_table):
     shape = direction.shape
     flat = lambda v: v.reshape(512, 1024)
-    product, sums = step_stage(
-        order_table, flat(direction), flat(residual), flat(noise_var), legendre, temporal)
-    outs = update(sums, flat(solution), flat(residual), flat(direction), product)
+    product, sums, direction, residual, solution = step_stage(
+        order_table, flat(direction), flat(residual), flat(solution), flat(noise_var), legendre,
+        temporal)
+    outs = update(sums, solution, residual, direction, product)
     return tuple(o.reshape(shape) for o in outs)
 
 

time: 117 us -> 119 us (1.017)
  local copies, waits for them, and re-layouts: 2.27 us -> 7.03 us
  Pallas kernels: 114 us -> 111 us
    unnamed x10, local copies, waits for them, and re-layouts: 2.27 us -> 7.03 us
    pallas_call x1, Pallas kernels: 111 us -> 108 us  [step_stage(): pl.pallas_call(step_kernel, out_shape=(shape, jax.ShapeDtypeStruct((8, 12...]
where the time goes in v3:
time: 119 us; the launch traced here: 118 us
  Pallas kernels  111 us (93%)
  local copies, waits for them, and re-layouts  7.03 us (6%)
    pallas_call x1, Pallas kernels, step_stage(): pl.pallas_call(step_kernel, out_shape=(shape, jax.ShapeDtypeStruct((8, 12...  108 us
    unnamed x10, local copies, waits for them, and re-layouts  7.03 us
    pallas_call x1, Pallas kernels, update(): pl.pallas_call(update_kernel, out_shape=(shape, shape, shape), in_specs=[...  3 us

profile of v3, /device:TPU:1, one launch (start us, length us, event | category | flops | bytes accessed | tf_op | source)
XLA Modules:
  0.0 118.2 jit_solution(16695145827367761675)
XLA Ops:
  0.6 107.6 %step_stage.1 = (f32[512,1024]{1,0:T(8,128)}, f32[8,128]{1,0:T(8,128)}, f32[512,1024]{1,0:T(8,128)}, f32[512,1024]{1,0:T(8,128)}, f32[512,1024]{1,0:T(8,128)}) custom-call(s32[512]{0:T(512)} %orders.1, f32[512,1024]{1,0:T(8,128)} %bitcast.7, f32[512,1024]{1,0:T(8,128)} %bitcast.8, f32[512,1024]{1,0:T(8,128)} %bitcast.9, f32[512,1024]{1,0:T(8,128)} %bitcast.10, ...), custom_call_target="tpu_custom_call" | custom-call | tf_op jit(solution)/shard_map/step_stage/pallas_call | solution.py:603
  108.2 0.0 copy-start
  108.2 1.6 %copy-done = f32[512,1024]{1,0:T(8,128)S(1)} copy-done((f32[512,1024]{1,0:T(8,128)S(1)}, f32[512,1024]{1,0:T(8,128)}, u32[]{:S(2)}) %copy-start) | copy-done | bytes 2097176
  109.8 0.0 copy-start.1
  109.8 1.6 %copy-done.1 = f32[512,1024]{1,0:T(8,128)S(1)} copy-done((f32[512,1024]{1,0:T(8,128)S(1)}, f32[512,1024]{1,0:T(8,128)}, u32[]{:S(2)}) %copy-start.1) | copy-done | bytes 2097176
  111.4 0.0 copy-start.2
  111.4 1.6 %copy-done.2 = f32[512,1024]{1,0:T(8,128)S(1)} copy-done((f32[512,1024]{1,0:T(8,128)S(1)}, f32[512,1024]{1,0:T(8,128)}, u32[]{:S(2)}) %copy-start.2) | copy-done | bytes 2097176
  113.0 0.0 copy-start.3
  113.0 1.6 %copy-done.3 = f32[512,1024]{1,0:T(8,128)S(1)} copy-done((f32[512,1024]{1,0:T(8,128)S(1)}, f32[512,1024]{1,0:T(8,128)}, u32[]{:S(2)}) %copy-start.3) | copy-done | bytes 2097176
  114.6 0.0 copy-start.4
  114.6 0.7 copy-done.4
  115.2 3.0 %update.1 = (f32[512,1024]{1,0:T(8,128)}, f32[512,1024]{1,0:T(8,128)}, f32[512,1024]{1,0:T(8,128)}) custom-call(f32[8,128]{1,0:T(8,128)S(1)} %copy-done.4, f32[512,1024]{1,0:T(8,128)S(1)} %copy-done.3, f32[512,1024]{1,0:T(8,128)S(1)} %copy-done.2, f32[512,1024]{1,0:T(8,128)S(1)} %copy-done.1, f32[512,1024]{1,0:T(8,128)S(1)} %copy-done), custom_call_target="tpu_custom_call" | custom-call | tf_op jit(solution)/shard_map/update/pallas_call | solution.py:686
Async XLA Ops:
  108.2 1.6 %copy-start = (f32[512,1024]{1,0:T(8,128)S(1)}, f32[512,1024]{1,0:T(8,128)}, u32[]{:S(2)}) copy-start(f32[512,1024]{1,0:T(8,128)} %get-tuple-element.15.product) | copy-start | bytes 6291460
  109.8 1.6 %copy-start.1 = (f32[512,1024]{1,0:T(8,128)S(1)}, f32[512,1024]{1,0:T(8,128)}, u32[]{:S(2)}) copy-start(f32[512,1024]{1,0:T(8,128)} %get-tuple-element.14.direction) | copy-start | bytes 6291460
  111.4 1.6 %copy-start.2 = (f32[512,1024]{1,0:T(8,128)S(1)}, f32[512,1024]{1,0:T(8,128)}, u32[]{:S(2)}) copy-start(f32[512,1024]{1,0:T(8,128)} %get-tuple-element.13.residual) | copy-start | bytes 6291460
  113.0 1.6 %copy-start.3 = (f32[512,1024]{1,0:T(8,128)S(1)}, f32[512,1024]{1,0:T(8,128)}, u32[]{:S(2)}) copy-start(f32[512,1024]{1,0:T(8,128)} %get-tuple-element.12.solution) | copy-start | bytes 6291460
  114.6 0.7 copy-start.4

commit v4 on v3

--- a/solution.py
+++ b/solution.py
@@ -16,6 +16,8 @@
 MESH = pl.DeviceIdType.MESH
 GROUPS = 4
 ORD = 8
+LAST = 2
+SLOT = (0, 1, None, 2)
 FIRST = (4, 5, 6, 0)
 VM = pl.BlockSpec(memory_space=pltpu.VMEM)
 
@@ -41,9 +43,9 @@
     return (col == moved).astype(F32).astype(BF)
 
 
-def step_kernel(orders, direction_in, residual_in, solution_in, noise_in, legendre_in, temporal_in,
-                product, sums, direction, residual, solution, noise, legendre, temporal, load, split,
-                rows, table, spectra, ring, full, part, leg, recv, blocks, mid, perm, coef, mixed, acc,
+def step_kernel(orders_in, direction_in, residual_in, solution_in, noise_in, legendre_in, temporal_in,
+                product, sums, direction, residual, solution, orders, noise, legendre, temporal, load,
+                split, rows, table, spectra, ring, full, leg, recv, blocks, mid, perm, coef, mixed, acc,
                 far_in, fin_in, last_far, last_fin, last, out, synth, stage, line, plane, in_send, in_recv, own_send, fwd_send, dup_send,
                 own_recv, fwd_recv, dup_recv, pair_send, pair_recv, far_send, far_recv, line_send,
                 line_recv, out_send, out_recv, sum_send, sum_recv, all_send, all_recv):
@@ -51,7 +53,8 @@
         pltpu.make_async_copy(src, dst, load.at[n])
         for n, (src, dst) in enumerate((
             (direction_in, direction), (legendre_in, legendre), (temporal_in, temporal),
-            (residual_in, residual), (noise_in, noise), (solution_in, solution)))
+            (residual_in, residual), (noise_in, noise), (solution_in, solution),
+            (orders_in, orders)))
     ]
     for copy in loads:
         copy.start()
@@ -116,17 +119,17 @@
                       out_recv.at[3 + n, k], {"blk_0": ty, "blk_1": tz})
 
     def last_far_copy(way):
-        return remote(last.at[0, pl.ds(way * 8, 8)], last_far.at[way], far_send.at[3, way],
-                      far_recv.at[3, way], side[way])
+        return remote(last.at[0, pl.ds(way * 8, 8)], last_far.at[way], far_send.at[LAST, way],
+                      far_recv.at[LAST, way], side[way])
 
     def last_line_copy(way):
-        return remote(last.at[1 + way], last_fin.at[way], line_send.at[3, way],
-                      line_recv.at[3, way], side[way])
+        return remote(last.at[1 + way], last_fin.at[way], line_send.at[LAST, way],
+                      line_recv.at[LAST, way], side[way])
 
     def out_copy(g, k):
         ty, tz = (y + k // 4) % 4, (z + k % 4) % 4
-        return remote(blocks.at[g, ty * 4 + tz], out.at[g, me], out_send.at[g, k],
-                      out_recv.at[g, k], {"blk_0": ty, "blk_1": tz})
+        return remote(blocks.at[SLOT[g], ty * 4 + tz], out.at[g, me], out_send.at[SLOT[g], k],
+                      out_recv.at[SLOT[g], k], {"blk_0": ty, "blk_1": tz})
 
     def hours(plane, who):
         return pl.ds(pl.multiple_of((plane * 2 + who) * 16, 16), 16)
@@ -151,15 +154,15 @@
     planes = (far, right, left, x)
 
     def pair_copy(g, n):
-        return remote(part.at[pl.ds(g * ORD, ORD), :, hours(planes[n], 1 - core), :], acc.at[g, n],
+        return remote(full.at[pl.ds(g * ORD, ORD), :, hours(planes[n], 1 - core), :], acc.at[g, n],
                       pair_send.at[g, n], pair_recv.at[g, n], peer)
 
     def far_copy(g, way):
-        return remote(acc.at[g, 0, pl.ds(way * half, half)], far_in.at[g, way],
+        return remote(acc.at[g, 0, pl.ds(way * half, half)], far_in.at[SLOT[g], way],
                       far_send.at[g, way], far_recv.at[g, way], side[way])
 
     def line_copy(g, way):
-        return remote(acc.at[g, 1 + way], fin_in.at[g, way], line_send.at[g, way],
+        return remote(acc.at[g, 1 + way], fin_in.at[SLOT[g], way], line_send.at[g, way],
                       line_recv.at[g, way], side[way])
 
     def regroup_in(n, g, plane_of):
@@ -252,6 +255,13 @@
 
         lax.fori_loop(0, ORD, analyse, 0, unroll=2)
 
+        for slot in range(4 if g == 0 else 5):
+            (dup_first(slot) if g == 0 else dup_copy(g, slot)).wait_send()
+        if g > 0:
+            for way in range(2):
+                own_copy(g, way).wait_send()
+                fwd_copy(g, way).wait_send()
+
         def mix(n, _):
             for k in range(16):
                 l = n * 16 + k
@@ -269,7 +279,7 @@
             value = lax.dot_general(
                 rows.astype(BF), leg[g * ORD + i], (((0,), (0,)), ((), ())),
                 preferred_element_type=F32)
-            part[g * ORD + i] = value.astype(BF).reshape(2, 128, 512)
+            full[g * ORD + i] = value.astype(BF).reshape(2, 128, 512)
             return 0
 
         lax.fori_loop(0, ORD, synthesise, 0, unroll=2)
@@ -281,12 +291,12 @@
             pair_copy(g, n).wait_recv()
 
             def step(i, _):
-                own = part[g * ORD + i, :, hours(planes[n], core), :]
+                own = full[g * ORD + i, :, hours(planes[n], core), :]
                 acc[g, n, i] = (acc[g, n, i].astype(F32) + own.astype(F32)).astype(BF)
                 return 0
 
             lax.fori_loop(0, ORD, step, 0)
-            if g == GROUPS - 1:
+            if g == LAST:
                 regroup_out(3 + n, lambda i, c: acc[g, n, i, c].astype(F32))
 
                 def send(k, _):
@@ -305,7 +315,7 @@
 
             def step(i, _):
                 acc[g, 1 + way, way * half + i] = (
-                    acc[g, 1 + way, way * half + i].astype(F32) + far_in[g, way, i].astype(F32)
+                    acc[g, 1 + way, way * half + i].astype(F32) + far_in[SLOT[g], way, i].astype(F32)
                 ).astype(BF)
                 return 0
 
@@ -337,15 +347,15 @@
     def depart(g):
         line_copy(g, 0).wait_recv()
         line_copy(g, 1).wait_recv()
-        regroup_out(g, lambda i, c: acc[g, 3, i, c].astype(F32) + fin_in[g, 0, i, c].astype(F32)
-                    + fin_in[g, 1, i, c].astype(F32))
+        regroup_out(SLOT[g], lambda i, c: acc[g, 3, i, c].astype(F32)
+                    + fin_in[SLOT[g], 0, i, c].astype(F32) + fin_in[SLOT[g], 1, i, c].astype(F32))
 
         def send(k, _):
             out_copy(g, k).start()
             return 0
 
         lax.fori_loop(1, 16, send, 0)
-        out[g, pl.ds(me, 1)] = blocks[g, pl.ds(me, 1)]
+        out[g, pl.ds(me, 1)] = blocks[SLOT[g], pl.ds(me, 1)]
 
     def last_arrived(n):
         def wait(k, _):
@@ -381,22 +391,11 @@
         low = jnp.minimum(value, 511 - value)
         return low + jnp.where(value == low, 0, 1024)
 
-    loads[0].wait()
-    lat, time = 32, 16
-    for q in range(8):
-        split[q * 512 : (q + 1) * 512, :] = direction[:, q * 128 : (q + 1) * 128]
-
-    def gather(t, _):
-        for q in range(8):
-            rows[pl.ds(pl.multiple_of(t * lat, lat), lat), q * 128 : (q + 1) * 128] = split[
-                pl.ds(q * 512 + t, lat, stride=time), :
-            ].astype(BF)
-        return 0
-
-    lax.fori_loop(0, time, gather, 0, unroll=2)
+    loads[6].wait()
     lane = lax.broadcasted_iota(jnp.int32, (4 * ORD, 128), 1)
     scale = 1.0 / math.sqrt(512.0)
-    for g in range(GROUPS):
+
+    def fill_group(g):
         def fill(n, _):
             m = jnp.concatenate([order_rows(n * 4 + k, g % 2) for k in range(4)], axis=0) % 1024
             m = m if g < 2 else 511 - m
@@ -412,6 +411,33 @@
             return 0
 
         lax.fori_loop(0, 4, fill, 0)
+
+    def send_in(g):
+        def send(k, _):
+            in_copy(g, k).start()
+            return 0
+
+        lax.fori_loop(1, 16, send, 0)
+        recv[g, pl.ds(me, 1)] = spectra[g, pl.ds(me, 1)]
+
+    fill_group(0)
+    fill_group(1)
+    loads[0].wait()
+    lat, time = 32, 16
+    for q in range(8):
+        split[q * 512 : (q + 1) * 512, :] = direction[:, q * 128 : (q + 1) * 128]
+
+    def gather(t, _):
+        for q in range(8):
+            rows[pl.ds(pl.multiple_of(t * lat, lat), lat), q * 128 : (q + 1) * 128] = split[
+                pl.ds(q * 512 + t, lat, stride=time), :
+            ].astype(BF)
+        return 0
+
+    lax.fori_loop(0, time, gather, 0, unroll=2)
+    for g in range(GROUPS):
+        if g >= 2:
+            fill_group(g)
         spectra[g] = lax.dot_general(
             table[g * 256 : (g + 1) * 256, :], rows[...], (((1,), (1,)), ((), ())),
             preferred_element_type=F32).astype(BF).reshape(16, 2 * ORD, 512)
@@ -422,18 +448,11 @@
             ring_copy(1).start()
             continue
 
-        def send_in(k, _):
-            in_copy(g, k).start()
-            return 0
-
-        lax.fori_loop(1, 16, send_in, 0)
-        recv[g, pl.ds(me, 1)] = spectra[g, pl.ds(me, 1)]
+        if g < 3:
+            send_in(g)
         if g == 1:
             send_first(3)
     perm[...] = lane_swap()
-    arrive(1)
-    forward_first()
-    arrive(2)
     degree = (x * 2 + core) * 64 + lax.broadcasted_iota(jnp.int32, (64, 512), 0)
     loads[1].wait()
     loads[2].wait()
@@ -447,34 +466,40 @@
             swap, low = entry >= 1024, entry % 1024
             leg[n] = jnp.where(degree >= low, jnp.where(swap, second, first), 0.0).astype(BF)
             leg[16 + n] = jnp.where(degree >= 511 - low, jnp.where(swap, first, second), 0.0).astype(BF)
+    forward_first()
+    arrive(1)
     far_first()
+    send_in(3)
+    arrive(2)
     arrive_first(3)
-    forward(1)
-    arrive(3)
     arrive_first(0)
     arrive_first(1)
+    forward(1)
     arrive_first(2)
+    arrive(3)
+    forward(2)
+    middle(0)
     forward_far(1)
-    middle(0)
-    forward(2)
     add_pair(0)
     middle(1)
     forward(3)
     forward_far(2)
     add_pair(1)
+    add_far(0)
     middle(2)
     forward_far(3)
-    add_far(0)
+    add_far(1)
     add_pair(2)
     middle(3)
-    add_far(1)
     add_pair(3)
     depart(0)
-    add_far(2)
     last_arrived(0)
     last_far_copy(0).start()
     last_far_copy(1).start()
+    add_far(3)
     depart(1)
+    last_add(0)
+    last_add(1)
 
     def arrived(g):
         def wait(k, _):
@@ -490,9 +515,6 @@
             value, table[first * 256 : (first + count) * 256, :], (((0,), (0,)), ((), ())),
             preferred_element_type=F32)
 
-    last_add(0)
-    last_add(1)
-    depart(2)
     arrived(0)
     arrived(1)
 
@@ -501,25 +523,26 @@
         return 0
 
     lax.fori_loop(0, 4, partial, 0)
+    depart(3)
     for n in range(3, 6):
         loads[n].wait()
     last_arrived(3)
-    arrived(2)
+    for way in range(2):
+        last_line_copy(way).wait_recv()
+
+    def total(j, _):
+        out[LAST, j] = (last[3, j].astype(F32) + last_fin[0, j].astype(F32)
+                        + last_fin[1, j].astype(F32)).astype(BF)
+        return 0
+
+    lax.fori_loop(0, 16, total, 0)
 
     def partial2(n, _):
         synth[pl.ds(pl.multiple_of(n * 128, 128), 128), :] += transform(2, 1, n)
         return 0
 
     lax.fori_loop(0, 4, partial2, 0)
-    for way in range(2):
-        last_line_copy(way).wait_recv()
-
-    def total(j, _):
-        out[3, j] = (last[3, j].astype(F32) + last_fin[0, j].astype(F32)
-                     + last_fin[1, j].astype(F32)).astype(BF)
-        return 0
-
-    lax.fori_loop(0, 16, total, 0)
+    arrived(3)
 
     def synthesis(n, _):
         block = synth[pl.ds(pl.multiple_of(n * 128, 128), 128), :] + transform(3, 1, n)
@@ -570,22 +593,19 @@
             if g == 0:
                 ring_copy(way).wait_send()
                 ring_forward(way).wait_send()
-            else:
-                own_copy(g, way).wait_send()
-                fwd_copy(g, way).wait_send()
-            if g == GROUPS - 1:
+            if g == LAST:
                 last_far_copy(way).wait_send()
                 last_line_copy(way).wait_send()
             else:
                 far_copy(g, way).wait_send()
                 line_copy(g, way).wait_send()
-        for slot in range(4 if g == 0 else 5):
-            (dup_first(slot) if g == 0 else dup_copy(g, slot)).wait_send()
 
     def finish(k, _):
         for g in range(1, GROUPS):
             in_copy(g, k).wait_send()
-            out_copy(g - 1, k).wait_send()
+            if g - 1 != LAST:
+                out_copy(g - 1, k).wait_send()
+        out_copy(3, k).wait_send()
         for n in range(4):
             in_first(n, k).wait_send()
             out_last(n, k).wait_send()
@@ -603,19 +623,19 @@
     return pl.pallas_call(
         step_kernel,
         out_shape=(shape, jax.ShapeDtypeStruct((8, 128), F32), shape, shape, shape),
-        in_specs=[pl.BlockSpec(memory_space=pltpu.SMEM)] + [hbm] * 6,
+        in_specs=[pl.BlockSpec(memory_space=pltpu.HBM)] + [hbm] * 6,
         out_specs=(VM,) * 5,
         scratch_shapes=[
+            pltpu.SMEM((512,), jnp.int32),
             grid,
             pltpu.VMEM((32, 64, 512), BF),
             pltpu.VMEM((64, 128, 128), F32),
-            dma((6,)),
+            dma((7,)),
             pltpu.VMEM((4096, 128), F32),
             pltpu.VMEM((512, 1024), BF),
             pltpu.VMEM((1024, 1024), BF),
             pltpu.VMEM((GROUPS, 16, 2 * ORD, 512), BF),
             pltpu.VMEM((3, 16, 2 * ORD, 512), BF),
-            pltpu.VMEM((32, 2, 128, 512), BF),
             pltpu.VMEM((32, 2, 128, 512), BF),
             pltpu.VMEM((32, 64, 512), BF),
             pltpu.VMEM((GROUPS + 3, 16, 2 * ORD, 512), BF),
@@ -639,7 +659,7 @@
             dma((8,)), dma((8,)), dma((16,)), dma((16,)),
         ],
         compiler_params=pltpu.CompilerParams(
-            collective_id=0, has_side_effects=True, vmem_limit_bytes=58 * 1024 * 1024),
+            collective_id=0, has_side_effects=True, vmem_limit_bytes=45 * 1024 * 1024),
         name="step_stage",
     )(orders, direction, residual, solution, noise, legendre, temporal)
 

time: 119 us -> 103 us (0.87)
  Pallas kernels: 111 us -> 102 us
  local copies, waits for them, and re-layouts: 7.03 us -> 0.67 us
    pallas_call x1, Pallas kernels: 108 us -> 98.8 us  [step_stage(): pl.pallas_call(step_kernel, out_shape=(shape, jax.ShapeDtypeStruct((8, 12...]
    unnamed x10 -> x2, local copies, waits for them, and re-layouts: 7.03 us -> 0.67 us
where the time goes in v4:
time: 103 us
  Pallas kernels  102 us (99%)
    pallas_call x1, Pallas kernels, step_stage(): pl.pallas_call(step_kernel, out_shape=(shape, jax.ShapeDtypeStruct((8, 12...  98.8 us
    pallas_call x1, Pallas kernels, update(): pl.pallas_call(update_kernel, out_shape=(shape, shape, shape), in_specs=[...  3 us

profile of v4, /device:TPU:1, one launch (start us, length us, event | category | flops | bytes accessed | tf_op | source)
XLA Modules:
  0.0 103.1 jit_solution(7061534460765860078)
XLA Ops:
  0.6 0.0 copy-start
  0.6 0.7 copy-done
  1.3 98.8 %step_stage.1 = (f32[512,1024]{1,0:T(8,128)S(1)}, f32[8,128]{1,0:T(8,128)S(1)}, f32[512,1024]{1,0:T(8,128)S(1)}, f32[512,1024]{1,0:T(8,128)S(1)}, f32[512,1024]{1,0:T(8,128)S(1)}) custom-call(s32[512]{0:T(512)S(1)} %copy-done, f32[512,1024]{1,0:T(8,128)} %bitcast.7, f32[512,1024]{1,0:T(8,128)} %bitcast.8, f32[512,1024]{1,0:T(8,128)} %bitcast.9, ...), custom_call_target="tpu_custom_call" | custom-call | tf_op jit(solution)/shard_map/step_stage/pallas_call | solution.py:623
  100.1 3.0 %update.1 = (f32[512,1024]{1,0:T(8,128)}, f32[512,1024]{1,0:T(8,128)}, f32[512,1024]{1,0:T(8,128)}) custom-call(f32[8,128]{1,0:T(8,128)S(1)} %get-tuple-element.11.sums, f32[512,1024]{1,0:T(8,128)S(1)} %get-tuple-element.12.solution, f32[512,1024]{1,0:T(8,128)S(1)} %get-tuple-element.13.residual, f32[512,1024]{1,0:T(8,128)S(1)} %get-tuple-element.14.direction, ...), custom_call_target="tpu_custom_call" | custom-call | tf_op jit(solution)/shard_map/update/pallas_call | solution.py:706
Async XLA Ops:
  0.6 0.7 copy-start

commit v5 on v4

--- a/solution.py
+++ b/solution.py
@@ -46,17 +46,17 @@
 def step_kernel(orders_in, direction_in, residual_in, solution_in, noise_in, legendre_in, temporal_in,
                 product, sums, direction, residual, solution, orders, noise, legendre, temporal, load,
                 split, rows, table, spectra, ring, full, leg, recv, blocks, mid, perm, coef, mixed, acc,
-                far_in, fin_in, last_far, last_fin, last, out, synth, stage, line, plane, in_send, in_recv, own_send, fwd_send, dup_send,
+                far_in, fin_in, last_far, last_fin, last, out, synth, rhat, nhat, tot, stage, line, plane, in_send, in_recv, own_send, fwd_send, dup_send,
                 own_recv, fwd_recv, dup_recv, pair_send, pair_recv, far_send, far_recv, line_send,
                 line_recv, out_send, out_recv, sum_send, sum_recv, all_send, all_recv):
     loads = [
         pltpu.make_async_copy(src, dst, load.at[n])
         for n, (src, dst) in enumerate((
-            (direction_in, direction), (legendre_in, legendre), (temporal_in, temporal),
+            (direction_in, direction), (legendre_in, legendre), (temporal_in.at[pl.ds(0, 4096)], synth),
             (residual_in, residual), (noise_in, noise), (solution_in, solution),
-            (orders_in, orders)))
+            (orders_in, orders), (temporal_in.at[pl.ds(4096, 4096)], split)))
     ]
-    for copy in loads:
+    for copy in loads[:7]:
         copy.start()
     y, z = lax.axis_index("blk_0"), lax.axis_index("blk_1")
     x, core = lax.axis_index("tm_0"), lax.axis_index("tm_1")
@@ -253,7 +253,7 @@
             coef[pl.ds(ORD * 64 + row, 64), :] = value[:, 128:]
             return 0
 
-        lax.fori_loop(0, ORD, analyse, 0, unroll=2)
+        lax.fori_loop(0, ORD, analyse, 0, unroll=4)
 
         for slot in range(4 if g == 0 else 5):
             (dup_first(slot) if g == 0 else dup_copy(g, slot)).wait_send()
@@ -268,7 +268,7 @@
                 rows = jnp.concatenate(
                     [coef[pl.ds(c * ORD * 64 + l, ORD, stride=64), :] for c in range(2)], axis=0)
                 mixed[pl.ds(pl.multiple_of(l * 16, 16), 16), :] = jnp.dot(
-                    rows.astype(BF), temporal[l].astype(BF), preferred_element_type=F32)
+                    rows.astype(BF), temporal[l], preferred_element_type=F32)
             return 0
 
         lax.fori_loop(0, 4, mix, 0)
@@ -282,7 +282,7 @@
             full[g * ORD + i] = value.astype(BF).reshape(2, 128, 512)
             return 0
 
-        lax.fori_loop(0, ORD, synthesise, 0, unroll=2)
+        lax.fori_loop(0, ORD, synthesise, 0, unroll=4)
         for n in range(4):
             pair_copy(g, n).start()
 
@@ -435,6 +435,7 @@
         return 0
 
     lax.fori_loop(0, time, gather, 0, unroll=2)
+    loads[7].start()
     for g in range(GROUPS):
         if g >= 2:
             fill_group(g)
@@ -456,6 +457,15 @@
     degree = (x * 2 + core) * 64 + lax.broadcasted_iota(jnp.int32, (64, 512), 0)
     loads[1].wait()
     loads[2].wait()
+    loads[7].wait()
+
+    def narrow(l, _):
+        part = pl.ds(pl.multiple_of(l * 128, 128), 128)
+        temporal[l] = synth[part, :].astype(BF)
+        temporal[32 + l] = split[part, :].astype(BF)
+        return 0
+
+    lax.fori_loop(0, 32, narrow, 0, unroll=2)
     for odd in range(2):
         entry_rows = order_rows(me, odd)
         for k in range(ORD):
@@ -466,6 +476,58 @@
             swap, low = entry >= 1024, entry % 1024
             leg[n] = jnp.where(degree >= low, jnp.where(swap, second, first), 0.0).astype(BF)
             leg[16 + n] = jnp.where(degree >= 511 - low, jnp.where(swap, first, second), 0.0).astype(BF)
+    def project(value, target):
+        for q in range(8):
+            split[q * 512 : (q + 1) * 512, :] = value(q)
+        lax.fori_loop(0, time, gather, 0, unroll=2)
+
+        def one(g, _):
+            target[g] = lax.dot_general(
+                table[pl.ds(pl.multiple_of(g * 256, 256), 256), :], rows[...],
+                (((1,), (1,)), ((), ())), preferred_element_type=F32,
+            ).astype(BF).reshape(16, 2 * ORD, 512)
+            return 0
+
+        lax.fori_loop(0, GROUPS, one, 0)
+
+    def local_sums():
+        def step(n, totals):
+            r8 = pl.ds(pl.multiple_of(n * 8, 8), 8)
+            nn, dp, rp, pp = totals
+            for q in range(8):
+                cols = slice(q * 128, (q + 1) * 128)
+                d, r = direction[r8, cols], residual[r8, cols]
+                e = noise[r8, cols] * d
+                nn, dp, rp, pp = nn + r * r, dp + d * e, rp + r * e, pp + e * e
+            return nn, dp, rp, pp
+
+        zero = jnp.zeros((8, 128), F32)
+        totals = lax.fori_loop(0, 64, step, (zero, zero, zero, zero), unroll=2)
+        for k in range(4):
+            tot[k] = totals[k]
+
+    def fold(v):
+        v = v[:8] + v[8:]
+        return (v[:, :128] + v[:, 128:256]) + (v[:, 256:384] + v[:, 384:])
+
+    def spectral_sums(g):
+        def step(o, totals):
+            dp, rp, pp = totals
+            value = out[g, o].astype(F32)
+            weighted = value
+            if g < 2:
+                low = jnp.concatenate([order_rows(o, g) % 1024] * 4, axis=1)
+                weighted = jnp.concatenate(
+                    [jnp.where(low == 0, 2.0 * value[:ORD], value[:ORD]), value[ORD:]], axis=0)
+            dp = dp + fold(spectra[g, o].astype(F32) * value)
+            rp = rp + fold(rhat[g, o].astype(F32) * value)
+            pp = pp + fold(value * (weighted + 2.0 * nhat[g, o].astype(F32)))
+            return dp, rp, pp
+
+        totals = lax.fori_loop(0, 16, step, (tot[1], tot[2], tot[3]))
+        for k in range(3):
+            tot[1 + k] = totals[k]
+
     forward_first()
     arrive(1)
     far_first()
@@ -498,8 +560,14 @@
     last_far_copy(1).start()
     add_far(3)
     depart(1)
+    for n in range(3, 6):
+        loads[n].wait()
+    project(lambda q: residual[:, q * 128 : (q + 1) * 128], rhat)
     last_add(0)
     last_add(1)
+    depart(3)
+    project(lambda q: noise[:, q * 128 : (q + 1) * 128] * direction[:, q * 128 : (q + 1) * 128], nhat)
+    local_sums()
 
     def arrived(g):
         def wait(k, _):
@@ -515,17 +583,9 @@
             value, table[first * 256 : (first + count) * 256, :], (((0,), (0,)), ((), ())),
             preferred_element_type=F32)
 
-    arrived(0)
-    arrived(1)
-
-    def partial(n, _):
-        synth[pl.ds(pl.multiple_of(n * 128, 128), 128), :] = transform(0, 2, n)
-        return 0
-
-    lax.fori_loop(0, 4, partial, 0)
-    depart(3)
-    for n in range(3, 6):
-        loads[n].wait()
+    for g in range(2):
+        arrived(g)
+        spectral_sums(g)
     last_arrived(3)
     for way in range(2):
         last_line_copy(way).wait_recv()
@@ -536,16 +596,18 @@
         return 0
 
     lax.fori_loop(0, 16, total, 0)
-
-    def partial2(n, _):
-        synth[pl.ds(pl.multiple_of(n * 128, 128), 128), :] += transform(2, 1, n)
-        return 0
-
-    lax.fori_loop(0, 4, partial2, 0)
+    spectral_sums(LAST)
     arrived(3)
+    spectral_sums(3)
+    for k in range(4):
+        stage[0, 2 * k : 2 * k + 2, :] = jnp.broadcast_to(
+            jnp.sum(tot[k], axis=0, keepdims=True), (2, 128))
+    for k in range(1, 8):
+        sum_copy(k).start()
+    line[pl.ds(x * 2 + core, 1)] = stage[0:1]
 
     def synthesis(n, _):
-        block = synth[pl.ds(pl.multiple_of(n * 128, 128), 128), :] + transform(3, 1, n)
+        block = transform(0, 4, n)
         for t in range(4):
             for q in range(8):
                 split[pl.ds(q * 512 + n * 4 + t, 32, stride=16), :] = (
@@ -553,32 +615,23 @@
         return 0
 
     lax.fori_loop(0, 4, synthesis, 0)
-
-    def combine(n, totals):
-        r8 = pl.ds(pl.multiple_of(n * 8, 8), 8)
-        nn, dp, rp, pp = totals
-        for q in range(8):
-            cols = slice(q * 128, (q + 1) * 128)
-            d, r = direction[r8, cols], residual[r8, cols]
-            p = split[pl.ds(pl.multiple_of(q * 512 + n * 8, 8), 8), :] + noise[r8, cols] * d
-            product[r8, cols] = p
-            nn, dp, rp, pp = nn + r * r, dp + d * p, rp + r * p, pp + p * p
-        return nn, dp, rp, pp
-
-    zero = jnp.zeros((8, 128), F32)
-    totals = lax.fori_loop(0, 64, combine, (zero, zero, zero, zero), unroll=2)
-    for k in range(4):
-        stage[0, 2 * k : 2 * k + 2, :] = jnp.broadcast_to(
-            jnp.sum(totals[k], axis=0, keepdims=True), (2, 128))
-    for k in range(1, 8):
-        sum_copy(k).start()
-    line[pl.ds(x * 2 + core, 1)] = stage[0:1]
     for k in range(1, 8):
         sum_copy(k).wait_recv()
     stage[1] = jnp.sum(line[...], axis=0)
     for k in range(1, 16):
         all_copy(k).start()
     plane[pl.ds(me, 1)] = stage[1:2]
+
+    def combine(n, _):
+        r8 = pl.ds(pl.multiple_of(n * 8, 8), 8)
+        for q in range(8):
+            cols = slice(q * 128, (q + 1) * 128)
+            product[r8, cols] = (
+                split[pl.ds(pl.multiple_of(q * 512 + n * 8, 8), 8), :]
+                + noise[r8, cols] * direction[r8, cols])
+        return 0
+
+    lax.fori_loop(0, 64, combine, 0, unroll=2)
     for k in range(1, 16):
         all_copy(k).wait_recv()
     sums[...] = jnp.sum(plane[...], axis=0)
@@ -629,8 +682,8 @@
             pltpu.SMEM((512,), jnp.int32),
             grid,
             pltpu.VMEM((32, 64, 512), BF),
-            pltpu.VMEM((64, 128, 128), F32),
-            dma((7,)),
+            pltpu.VMEM((64, 128, 128), BF),
+            dma((8,)),
             pltpu.VMEM((4096, 128), F32),
             pltpu.VMEM((512, 1024), BF),
             pltpu.VMEM((1024, 1024), BF),
@@ -651,7 +704,10 @@
             pltpu.VMEM((2, 16, 2 * ORD, 512), BF),
             pltpu.VMEM((4, 16, 2 * ORD, 512), BF),
             pltpu.VMEM((GROUPS, 16, 2 * ORD, 512), BF),
-            grid,
+            pltpu.VMEM((4096, 128), F32),
+            pltpu.VMEM((GROUPS, 16, 2 * ORD, 512), BF),
+            pltpu.VMEM((GROUPS, 16, 2 * ORD, 512), BF),
+            pltpu.VMEM((4, 8, 128), F32),
             pltpu.VMEM((2, 8, 128), F32),
             pltpu.VMEM((8, 8, 128), F32),
             pltpu.VMEM((16, 8, 128), F32),
@@ -719,7 +775,7 @@
     flat = lambda v: v.reshape(512, 1024)
     product, sums, direction, residual, solution = step_stage(
         order_table, flat(direction), flat(residual), flat(solution), flat(noise_var), legendre,
-        temporal)
+        temporal.reshape(8192, 128))
     outs = update(sums, solution, residual, direction, product)
     return tuple(o.reshape(shape) for o in outs)
 

time: 103 us -> 101 us (0.981)
  Pallas kernels: 102 us -> 99.8 us
    pallas_call x1, Pallas kernels: 98.8 us -> 96.8 us  [step_stage(): pl.pallas_call(step_kernel, out_shape=(shape, jax.ShapeDtypeStruct((8, 12...]
where the time goes in v5:
time: 101 us
  Pallas kernels  99.8 us (99%)
    pallas_call x1, Pallas kernels, step_stage(): pl.pallas_call(step_kernel, out_shape=(shape, jax.ShapeDtypeStruct((8, 12...  96.8 us
    pallas_call x1, Pallas kernels, update(): pl.pallas_call(update_kernel, out_shape=(shape, shape, shape), in_specs=[...  3 us

profile of v5, /device:TPU:1, one launch (start us, length us, event | category | flops | bytes accessed | tf_op | source)
XLA Modules:
  0.0 101.3 jit_solution(14978052519916668125)
XLA Ops:
  0.6 0.0 copy-start
  0.6 0.7 copy-done
  1.3 96.8 %step_stage.1 = (f32[512,1024]{1,0:T(8,128)S(1)}, f32[8,128]{1,0:T(8,128)S(1)}, f32[512,1024]{1,0:T(8,128)S(1)}, f32[512,1024]{1,0:T(8,128)S(1)}, f32[512,1024]{1,0:T(8,128)S(1)}) custom-call(s32[512]{0:T(512)S(1)} %copy-done, f32[512,1024]{1,0:T(8,128)} %bitcast.9, f32[512,1024]{1,0:T(8,128)} %bitcast.10, f32[512,1024]{1,0:T(8,128)} %bitcast.11, ...), custom_call_target="tpu_custom_call" | custom-call | tf_op jit(solution)/shard_map/step_stage/pallas_call | solution.py:676
  98.2 3.0 %update.1 = (f32[512,1024]{1,0:T(8,128)}, f32[512,1024]{1,0:T(8,128)}, f32[512,1024]{1,0:T(8,128)}) custom-call(f32[8,128]{1,0:T(8,128)S(1)} %get-tuple-element.11.sums, f32[512,1024]{1,0:T(8,128)S(1)} %get-tuple-element.12.solution, f32[512,1024]{1,0:T(8,128)S(1)} %get-tuple-element.13.residual, f32[512,1024]{1,0:T(8,128)S(1)} %get-tuple-element.14.direction, ...), custom_call_target="tpu_custom_call" | custom-call | tf_op jit(solution)/shard_map/update/pallas_call | solution.py:762
Async XLA Ops:
  0.6 0.7 copy-start

commit v6 on v5

--- a/solution.py
+++ b/solution.py
@@ -56,7 +56,13 @@
             (residual_in, residual), (noise_in, noise), (solution_in, solution),
             (orders_in, orders), (temporal_in.at[pl.ds(4096, 4096)], split)))
     ]
-    for copy in loads[:7]:
+    chunks = [
+        pltpu.make_async_copy(
+            direction_in.at[:, pl.ds(q * 128, 128)], split.at[pl.ds(q * 512, 512)], load.at[8 + q])
+        for q in range(8)
+    ]
+    loads[6].start()
+    for copy in chunks + loads[:6]:
         copy.start()
     y, z = lax.axis_index("blk_0"), lax.axis_index("blk_1")
     x, core = lax.axis_index("tm_0"), lax.axis_index("tm_1")
@@ -422,10 +428,9 @@
 
     fill_group(0)
     fill_group(1)
-    loads[0].wait()
     lat, time = 32, 16
-    for q in range(8):
-        split[q * 512 : (q + 1) * 512, :] = direction[:, q * 128 : (q + 1) * 128]
+    for copy in chunks:
+        copy.wait()
 
     def gather(t, _):
         for q in range(8):
@@ -534,6 +539,9 @@
     send_in(3)
     arrive(2)
     arrive_first(3)
+    for n in (0, 3, 4, 5):
+        loads[n].wait()
+    project(lambda q: residual[:, q * 128 : (q + 1) * 128], rhat)
     arrive_first(0)
     arrive_first(1)
     forward(1)
@@ -560,14 +568,11 @@
     last_far_copy(1).start()
     add_far(3)
     depart(1)
-    for n in range(3, 6):
-        loads[n].wait()
-    project(lambda q: residual[:, q * 128 : (q + 1) * 128], rhat)
+    project(lambda q: noise[:, q * 128 : (q + 1) * 128] * direction[:, q * 128 : (q + 1) * 128], nhat)
+    local_sums()
     last_add(0)
     last_add(1)
     depart(3)
-    project(lambda q: noise[:, q * 128 : (q + 1) * 128] * direction[:, q * 128 : (q + 1) * 128], nhat)
-    local_sums()
 
     def arrived(g):
         def wait(k, _):
@@ -683,7 +688,7 @@
             grid,
             pltpu.VMEM((32, 64, 512), BF),
             pltpu.VMEM((64, 128, 128), BF),
-            dma((8,)),
+            dma((16,)),
             pltpu.VMEM((4096, 128), F32),
             pltpu.VMEM((512, 1024), BF),
             pltpu.VMEM((1024, 1024), BF),

time: 101 us -> 100 us (0.990)
  Pallas kernels: 99.8 us -> 98.6 us
    pallas_call x1, Pallas kernels: 96.8 us -> 95.5 us  [step_stage(): pl.pallas_call(step_kernel, out_shape=(shape, jax.ShapeDtypeStruct((8, 12...]
where the time goes in v6:
time: 100 us
  Pallas kernels  98.6 us (99%)
    pallas_call x1, Pallas kernels, step_stage(): pl.pallas_call(step_kernel, out_shape=(shape, jax.ShapeDtypeStruct((8, 12...  95.5 us
    pallas_call x1, Pallas kernels, update(): pl.pallas_call(update_kernel, out_shape=(shape, shape, shape), in_specs=[...  3 us

profile of v6, /device:TPU:1, one launch (start us, length us, event | category | flops | bytes accessed | tf_op | source)
XLA Modules:
  0.0 100.0 jit_solution(8944610532162237779)
XLA Ops:
  0.6 0.0 copy-start
  0.6 0.7 copy-done
  1.3 95.5 %step_stage.1 = (f32[512,1024]{1,0:T(8,128)S(1)}, f32[8,128]{1,0:T(8,128)S(1)}, f32[512,1024]{1,0:T(8,128)S(1)}, f32[512,1024]{1,0:T(8,128)S(1)}, f32[512,1024]{1,0:T(8,128)S(1)}) custom-call(s32[512]{0:T(512)S(1)} %copy-done, f32[512,1024]{1,0:T(8,128)} %bitcast.9, f32[512,1024]{1,0:T(8,128)} %bitcast.10, f32[512,1024]{1,0:T(8,128)} %bitcast.11, ...), custom_call_target="tpu_custom_call" | custom-call | tf_op jit(solution)/shard_map/step_stage/pallas_call | solution.py:681
  96.9 3.0 %update.1 = (f32[512,1024]{1,0:T(8,128)}, f32[512,1024]{1,0:T(8,128)}, f32[512,1024]{1,0:T(8,128)}) custom-call(f32[8,128]{1,0:T(8,128)S(1)} %get-tuple-element.11.sums, f32[512,1024]{1,0:T(8,128)S(1)} %get-tuple-element.12.solution, f32[512,1024]{1,0:T(8,128)S(1)} %get-tuple-element.13.residual, f32[512,1024]{1,0:T(8,128)S(1)} %get-tuple-element.14.direction, ...), custom_call_target="tpu_custom_call" | custom-call | tf_op jit(solution)/shard_map/update/pallas_call | solution.py:767
Async XLA Ops:
  0.6 0.7 copy-start
